TPU v7x, 256 devices: a whole 4x4x8 slice. The times are simulated.
256 devices in a mesh: mb: 8 (over z), tp: 8 (over y, core), dp: 4 (over x).
Axes of the slice: x: 4, y: 4, z: 8, core: 2. Of those that a mesh axis runs over, the one named last changes fastest.
Arguments:
- hidden: bfloat16 [4, 16, 512, 7168], P('dp', 'mb', None, 'tp'), may hold values from -6 to 6
- latent: bfloat16 [4, 16, 512, 512], P('dp', 'mb', None, 'tp'), may hold values from -6 to 6
- out_grad: bfloat16 [4, 16, 512, 16384], P('dp', 'mb', None, 'tp'), may hold values from -0.059814453 to 0.059814453
- up_weight: bfloat16 [512, 16384], P(None, 'tp'), may hold values from -0.046875 to 0.046875
- mb_tokens: int32 [4, 16], P('dp'), may hold values from 128 to 512, as said below
- slot_mb: int32 [4, 16], P('dp', 'mb'), may hold values from 0 to 15, each once within a row
Outputs:
- up_grad: float32 [512, 16384], P(('mb', 'dp'), 'tp')
- running_down: float32 [8, 7168, 512], P('mb', 'tp', 'dp')
Inputs may be any that keep to these rules, and one draw needn't show every extreme that they name: `mb_tokens`: each count is a multiple of 128; in every group some microbatch has exactly 512 tokens. `slot_mb`: each row is a permutation of the microbatch numbers.
All inputs are finite; a program needn't handle non-finite values.
Results may differ from a plain program's by a relative error of at most 0.005.
Values may be sent and summed in bfloat16 or wider, within the bound.
A program may use at most 128 MiB of HBM per device.

v0:
```python
import jax
import jax.numpy as jnp
from jax import lax
from jax.sharding import PartitionSpec as P


def copy_for_each(value, axis):
    copies = jnp.broadcast_to(value, (lax.axis_size(axis), *value.shape))
    return lax.all_to_all(copies, axis, split_axis=0, concat_axis=0, tiled=True)


def laid_out(blocks, dim):
    blocks = jnp.moveaxis(blocks, 0, dim)
    dims = blocks.shape
    return blocks.reshape(*dims[:dim], dims[dim] * dims[dim + 1], *dims[dim + 2 :])


def gathered_copies(value, axis, dim):
    blocks = copy_for_each(value, axis)
    return laid_out(blocks, dim)


def rows_for(lines, length):
    spare = -lines.shape[0] % length
    if not spare:
        return lines
    return jnp.concatenate([lines, jnp.zeros((spare, *lines.shape[1:]), lines.dtype)])


def total_of(value, axis):
    lines = value.reshape(-1, *value.shape[1:][-1:])
    padded = rows_for(lines, lax.axis_size(axis))
    own = lax.psum_scatter(padded, axis, scatter_dimension=0, tiled=True)
    whole = lax.all_gather(own, axis, axis=0, tiled=True)
    return whole[: len(lines)].reshape(value.shape)


def split_up(value, dim, length):
    dims = value.shape
    blocks = value.reshape(*dims[:dim], length, dims[dim] // length, *dims[dim + 1 :])
    return jnp.moveaxis(blocks, dim, 0)


def summed_on_arrival(value, axis, dim):
    blocks = split_up(value, dim, lax.axis_size(axis))
    arrived = lax.all_to_all(blocks, axis, split_axis=0, concat_axis=0, tiled=True)
    return arrived.sum(axis=0)


def local(hidden, latent, out_grad, up_weight, mb_tokens, slot_mb):
    slot_count = hidden.shape[1]
    capacity = hidden.shape[2]
    micro_count = mb_tokens.shape[1]
    row_total = slot_count * capacity
    slot_ids = slot_mb[0]
    lookup = slot_ids[:, None] == jnp.arange(micro_count, dtype=jnp.int32)[None, :]
    counts = jnp.sum(jnp.where(lookup, mb_tokens[0][None, :], 0), axis=1)
    valid_rows = jnp.arange(capacity, dtype=jnp.int32)[None, :] < counts[:, None]
    masked_grads = jnp.where(valid_rows[:, :, None], out_grad[0], jnp.zeros((), out_grad.dtype))
    masked_grads = masked_grads.reshape(row_total, -1)
    factors = gathered_copies(latent[0].reshape(row_total, -1), "tp", 1)
    partial_latent = lax.dot_general(
        masked_grads, up_weight, (((1,), (1,)), ((), ())), preferred_element_type=jnp.float32
    )
    latent_grad = total_of(partial_latent, "tp").astype(jnp.bfloat16)
    owner_part = lax.psum_scatter(
        lax.dot_general(
            factors, masked_grads, (((0,), (0,)), ((), ())), preferred_element_type=jnp.float32
        ),
        "mb",
        scatter_dimension=0,
        tiled=True,
    )
    up_grad = summed_on_arrival(owner_part, "dp", 0)
    hidden_rows = hidden[0].reshape(row_total, -1)
    down_term = lax.dot_general(
        hidden_rows, latent_grad, (((0,), (0,)), ((), ())), preferred_element_type=jnp.float32
    )
    down_share = summed_on_arrival(down_term, "dp", 1)
    own_index = lax.axis_index("mb")
    shard_rows = lax.all_gather(down_share[None], "mb", axis=0, tiled=True)
    positions = jnp.arange(shard_rows.shape[0], dtype=jnp.int32)
    weights_in = (positions <= own_index).astype(jnp.float32)
    running = jnp.einsum("k,kdr->dr", weights_in, shard_rows)
    return (up_grad, running[None])


def solution(mesh):
    return jax.shard_map(
        local,
        mesh=mesh,
        in_specs=(
            P("dp", "mb", None, "tp"),
            P("dp", "mb", None, "tp"),
            P("dp", "mb", None, "tp"),
            P(None, "tp"),
            P("dp", None),
            P("dp", "mb"),
        ),
        out_specs=(P(("mb", "dp"), "tp"), P("mb", "tp", "dp")),
        check_vma=False,
    )
```

profile of v0, /device:TPU:16, one launch (start us, length us, event | category | flops | bytes accessed | tf_op | source)
XLA Modules:
  0.0 198.7 jit_solution(7407583883337681670)
XLA Ops:
  8.1 1.0 fusion.5
  9.1 0.1 iota_compare_fusion
  9.2 2.5 %bitcast_select_fusion = bf16[1024,2048]{1,0:T(8,128)(2,1)S(1)} fusion(bf16[1,2,512,2048]{3,2,1,0:T(8,128)(2,1)} %param.8, pred[1024]{0:T(1024)(128)(4,1)S(1)} %lt.24), kind=kLoop, calls=%fused_computation | loop fusion | flops 2097152 | bytes 8389632 | tf_op jit(solution)/shard_map/jit(_where)/select_n | solution.py:59
  11.7 3.7 %fusion.8 = f32[1024,512]{1,0:T(8,128)} fusion(bf16[1024,2048]{1,0:T(8,128)(2,1)S(1)} %bitcast_select_fusion, bf16[512,2048]{1,0:T(8,128)(2,1)S(1)} %copy-done), kind=kOutput, calls=%fused_computation.13 | convolution fusion | flops 2147483648 | bytes 8388608 | tf_op jit(solution)/shard_map/dot_general | solution.py:62
  15.5 34.3 %reduce-scatter.5.cloned.1.call-done = f32[128,512]{1,0:T(8,128)} async-done(((f32[1024,512]{1,0:T(8,128)}), f32[128,512]{1,0:T(8,128)}) %reduce-scatter.5.cloned.1.call-update) | async-done | bytes 262160 | tf_op jit(solution)/shard_map/reduce_scatter | solution.py:33
  49.9 0.1 copy.12
  50.1 1.1 broadcast_in_dim.48
  51.2 8.9 %all-to-all-start = ((bf16[8,1024,64]{1,2,0:T(8,128)(2,1)}), bf16[8,1024,64]{1,2,0:T(8,128)(2,1)S(1)}, u32[]{:S(2)}, u32[]{:S(2)}) async-start(bf16[8,1024,64]{1,2,0:T(8,128)(2,1)} %broadcast_in_dim.48), calls=%async_computation | async-start | bytes 2097152 | tf_op jit(solution)/shard_map/all_to_all | solution.py:9
  60.1 4.5 %broadcast_select_fusion = bf16[1,2,512,2048]{3,2,1,0:T(8,128)(2,1)} fusion(bf16[1,2,512,2048]{3,2,1,0:T(8,128)(2,1)} %param.8, pred[2,512]{1,0:T(4,128)(4,1)S(1)} %iota_compare_fusion), kind=kLoop, calls=%fused_computation.1 | loop fusion | flops 2097152 | bytes 8389632 | tf_op jit(solution)/shard_map/jit(_where)/select_n | solution.py:59
  64.6 12.1 %all-to-all-done = bf16[8,1024,64]{1,2,0:T(8,128)(2,1)S(1)} async-done(((bf16[8,1024,64]{1,2,0:T(8,128)(2,1)}), bf16[8,1024,64]{1,2,0:T(8,128)(2,1)S(1)}, u32[]{:S(2)}, u32[]{:S(2)}) %all-to-all-start) | async-done | bytes 1048608 | tf_op jit(solution)/shard_map/all_to_all | solution.py:9
  76.7 6.6 %convolution_bitcast_fusion = f32[512,2048]{0,1:T(8,128)} fusion(bf16[1024,2048]{1,0:T(8,128)(2,1)} %bitcast.38, bf16[1024,512]{0,1:T(8,128)(2,1)S(1)} %bitcast.41), kind=kOutput, calls=%fused_computation.2 | convolution fusion | flops 2147483648 | bytes 9437184 | tf_op jit(solution)/shard_map/dot_general | solution.py:67
  83.3 5.4 %copy.15 = f32[512,2048]{1,0:T(8,128)} copy(f32[512,2048]{0,1:T(8,128)} %convolution_bitcast_fusion) | data formatting | bytes 8388608
  88.7 0.0 all-gather.6.cloned.1.call-start
  88.8 3.4 %fusion = f32[512,896]{1,0:T(8,128)S(1)} fusion(bf16[1024,896]{1,0:T(8,128)(2,1)} %bitcast.45, f32[1024,512]{1,0:T(8,128)} %all-gather.4.cloned.1.call-done), kind=kOutput, calls=%fused_computation.3 | convolution fusion | flops 940048384 | bytes 5767168 | tf_op jit(solution)/shard_map/dot_general | solution.py:76
  92.2 27.2 %all_to_all.15 = f32[4,896,128]{1,2,0:T(8,128)} all-to-all(f32[4,896,128]{1,2,0:T(8,128)S(1)} %bitcast.40), channel_id=1, replica_groups=mesh['mb'=8,'tp'=8,'dp'=4] {'dp'}, dimensions={0} | all-to-all | bytes 3670016 | tf_op jit(solution)/shard_map/all_to_all | solution.py:46
  119.4 2.4 %reduce_sum.29 = bf16[896,128]{0,1:T(8,128)(2,1)} reduce(f32[4,896,128]{1,2,0:T(8,128)} %all_to_all.15, f32[]{:T(128)} %constant.4.clone.1), dimensions={0}, to_apply=%region_4.5 | reduce | flops 344064 | bytes 2064388 | tf_op jit(solution)/shard_map/reduce_sum | solution.py:47
  121.8 24.7 %reduce-scatter.7.cloned.1.call-done = f32[64,2048]{1,0:T(8,128)} async-done(((f32[512,2048]{1,0:T(8,128)}), f32[64,2048]{1,0:T(8,128)}) %reduce-scatter.7.cloned.1.call-update) | async-done | bytes 524304 | tf_op jit(solution)/shard_map/reduce_scatter | solution.py:66
  146.5 4.3 %all-to-all-start.1 = ((f32[4,16,2048]{2,1,0:T(8,128)}), f32[4,16,2048]{2,1,0:T(8,128)S(1)}, u32[]{:S(2)}, u32[]{:S(2)}) async-start(f32[4,16,2048]{2,1,0:T(8,128)} %bitcast.43), calls=%async_computation.1 | async-start | bytes 1048576 | tf_op jit(solution)/shard_map/all_to_all | solution.py:46
  150.8 9.4 %all-to-all-done.1 = f32[4,16,2048]{2,1,0:T(8,128)S(1)} async-done(((f32[4,16,2048]{2,1,0:T(8,128)}), f32[4,16,2048]{2,1,0:T(8,128)S(1)}, u32[]{:S(2)}, u32[]{:S(2)}) %all-to-all-start.1) | async-done | bytes 524320 | tf_op jit(solution)/shard_map/all_to_all | solution.py:46
  160.1 0.7 reduce_sum.28
  160.8 26.9 %all-gather.6.cloned.1.call-done = bf16[7168,128]{0,1:T(8,128)(2,1)} async-done(((bf16[896,128]{0,1:T(8,128)(2,1)}), bf16[7168,128]{0,1:T(8,128)(2,1)}) %all-gather.6.cloned.1.call-update) | async-done | bytes 1835024 | tf_op jit(solution)/shard_map/all_gather | solution.py:81
  187.7 1.8 copy.18
  189.5 0.6 fusion.2
  190.2 1.1 copy.14
  (14 shorter events, 0.2 us)
Async XLA Ops:
  8.0 3.7 %copy-start = (bf16[512,2048]{1,0:T(8,128)(2,1)S(1)}, bf16[512,2048]{1,0:T(8,128)(2,1)}, u32[]{:S(2)}) copy-start(bf16[512,2048]{1,0:T(8,128)(2,1)} %param.9) | copy-start | bytes 6291460
  8.0 41.9 %reduce-scatter.5.cloned.1.call-start = ((), (), s32[]{:S(2)}) async-start(), calls=%async_computation.5 | async-start | bytes 2359296 | tf_op jit(solution)/shard_map/reduce_scatter | solution.py:33
  15.4 34.4 %copy-start.1 = (bf16[1,2,512,64]{2,3,1,0:T(8,128)(2,1)S(1)}, bf16[1,2,512,64]{2,3,1,0:T(8,128)(2,1)}, u32[]{:S(2)}) copy-start(bf16[1,2,512,64]{2,3,1,0:T(8,128)(2,1)} %param.7) | copy-start | bytes 393220
  15.5 73.3 %all-gather.4.cloned.1.call-start = ((), (), s32[]{:S(2)}) async-start(), calls=%async_computation.6 | async-start | bytes 2359296 | tf_op jit(solution)/shard_map/all_gather | solution.py:34
  51.2 25.5 %all-to-all-start = ((bf16[8,1024,64]{1,2,0:T(8,128)(2,1)}), bf16[8,1024,64]{1,2,0:T(8,128)(2,1)S(1)}, u32[]{:S(2)}, u32[]{:S(2)}) async-start(bf16[8,1024,64]{1,2,0:T(8,128)(2,1)} %broadcast_in_dim.48), calls=%async_computation | async-start | bytes 2097152 | tf_op jit(solution)/shard_map/all_to_all | solution.py:9
  60.1 86.4 %reduce-scatter.7.cloned.1.call-start = ((), (), s32[]{:S(2)}) async-start(), calls=%async_computation.8 | async-start | bytes 4718592 | tf_op jit(solution)/shard_map/reduce_scatter | solution.py:66
  88.7 99.0 %all-gather.6.cloned.1.call-start = ((), (), s32[]{:S(2)}) async-start(), calls=%async_computation.7 | async-start | bytes 2064384 | tf_op jit(solution)/shard_map/all_gather | solution.py:81
  146.5 13.6 %all-to-all-start.1 = ((f32[4,16,2048]{2,1,0:T(8,128)}), f32[4,16,2048]{2,1,0:T(8,128)S(1)}, u32[]{:S(2)}, u32[]{:S(2)}) async-start(f32[4,16,2048]{2,1,0:T(8,128)} %bitcast.43), calls=%async_computation.1 | async-start | bytes 1048576 | tf_op jit(solution)/shard_map/all_to_all | solution.py:46
Sparse Core Ops, SparseCore 0:
  15.6 34.2 reduce-scatter.4
  51.7 32.8 all-gather.3
Sparse Core Ops, SparseCore 1:
  88.8 57.7 reduce-scatter.6
  148.8 38.9 all-gather.5
where the time goes:
time: 199 us
  waiting for transfers between devices  107 us (54%)
  blocking collectives  27.2 us (14%)
  between operations  15.6 us (8%)
  matrix products  14.4 us (7%)
  starting transfers between devices  13.3 us (7%)
  other arithmetic  11.2 us (6%)
  local copies, waits for them, and re-layouts  9.61 us (5%)
    reduce_scatter x1, waiting for transfers between devices, total_of(): own = lax.psum_scatter(padded, axis, scatter_dimension=0, tiled=True)  34.3 us
    all_to_all x1, blocking collectives, summed_on_arrival(): lax.all_to_all(blocks, axis, split_axis=0, concat_axis=0, tiled=True)  27.2 us
    all_gather x1, waiting for transfers between devices, local(): shard_rows = lax.all_gather(down_share[None], 'mb', axis=0, tiled=True)  26.9 us
    reduce_scatter x1, waiting for transfers between devices, local(): lax.psum_scatter(lax.dot_general(factors, masked_grads, (((0,), (0,)), ((...  24.7 us
    all_to_all x1, waiting for transfers between devices, copy_for_each(): return lax.all_to_all(copies, axis, split_axis=0, concat_axis=0, tiled=True)  12.1 us
    all_to_all x1, waiting for transfers between devices, summed_on_arrival(): lax.all_to_all(blocks, axis, split_axis=0, concat_axis=0, tiled=True)  9.36 us
    all_to_all x1, starting transfers between devices, copy_for_each(): return lax.all_to_all(copies, axis, split_axis=0, concat_axis=0, tiled=True)  8.94 us
    unnamed x8, local copies, waits for them, and re-layouts  7.36 us
  transfers between devices with their start and end apart: 6, of which 5 were waited for; matrix products, arithmetic and copies ran while one was open for 12% of the time, Pallas kernels for 0%

commit v1 on v0

v1 whole, which is shorter than its diff:
```python
import functools

import jax
import jax.numpy as jnp
from jax import lax
from jax.experimental import pallas as pl
from jax.experimental.pallas import tpu as pltpu
from jax.sharding import PartitionSpec as P

MESH = pl.DeviceIdType.MESH
F32 = jnp.float32
BF16 = jnp.bfloat16
NT = (((1,), (1,)), ((), ()))
NN = (((1,), (0,)), ((), ()))
NH = 2
NU = 4


def dot(a, b, dims):
    return lax.dot_general(a, b, dims, preferred_element_type=F32)


class Sems:
    def __init__(self, send, recv):
        self.send, self.recv, self.used = send, recv, 0

    def take(self):
        at = self.used
        self.used += 1
        return self.send.at[at], self.recv.at[at]


def kernel(
    n_z, n_y, n_x,
    hidden, latent, out_grad, weight, tokens, slots,
    up_out, down_out,
    lat_v, h_v, g_v, w_v, lat_all,
    pair_s, pair_r, lg_s, lg_b, lg_far, lg_near, lg_all,
    d_s, d_b, d_far, d_near, zs_d, zr_d, po_d, rf_d,
    u_b, u_far, u_near, zs_u, zr_u,
    load, send, recv,
):
    z = lax.axis_index("mb")
    tp = lax.axis_index("tp")
    x = lax.axis_index("dp")
    y, c = tp // 2, tp % 2
    oc = 1 - c
    cap = g_v.shape[1]
    blk = cap // n_y
    rows_h = lg_all.shape[1]
    rx = rows_h // n_x
    width = h_v.shape[1]
    columns = g_v.shape[2]
    nq = columns // NU

    def tp_of(row, core):
        return lax.rem(row + 2 * n_y, n_y) * 2 + core

    y_up, y_dn, y_far = tp_of(y + 1, c), tp_of(y - 1, c), tp_of(y + 2, c)
    x_up, x_dn, x_far = lax.rem(x + 1, n_x), lax.rem(x + n_x - 1, n_x), lax.rem(x + 2, n_x)
    partner = tp_of(y, oc)
    peers = [{"tp": partner}, {"tp": y_up}, {"tp": y_dn}, {"dp": x_up}, {"dp": x_dn}]
    z_peers = [lax.rem(z + d, n_z) for d in range(1, n_z)]
    peers += [{"mb": p} for p in z_peers]

    loads = []

    def fetch(src, dst):
        copy = pltpu.make_async_copy(src, dst, load.at[len(loads)])
        copy.start()
        loads.append(copy)
        return copy

    barrier = pltpu.get_barrier_semaphore()
    for peer in peers:
        pl.semaphore_signal(barrier, inc=1, device_id=peer, device_id_type=MESH)
    get_lat = fetch(latent, lat_v)
    get_w = [fetch(weight.at[:, 0], w_v.at[0])]
    get_g_other = fetch(out_grad.at[oc], g_v.at[oc])
    get_g_own = fetch(out_grad.at[c], g_v.at[c])
    get_w += [fetch(weight.at[:, h], w_v.at[h]) for h in range(1, NH)]
    get_h = fetch(hidden, h_v)

    sent = []
    sems = Sems(send, recv)

    def ship(src, dst, device, pair):
        copy = pltpu.make_async_remote_copy(
            src_ref=src, dst_ref=dst, send_sem=pair[0], recv_sem=pair[1],
            device_id=device, device_id_type=MESH,
        )
        copy.start()
        sent.append(copy)

    def arrive(dst, pair):
        pltpu.make_async_remote_copy(
            src_ref=dst, dst_ref=dst, send_sem=pair[0], recv_sem=pair[1],
            device_id={"tp": partner}, device_id_type=MESH,
        ).wait_recv()

    count = [tokens[0, slots[0, s]] for s in range(2)]

    get_lat.wait()
    n_lat = lat_v.shape[1]
    eye = (
        lax.broadcasted_iota(jnp.int32, (n_lat, n_lat), 0)
        == lax.broadcasted_iota(jnp.int32, (n_lat, n_lat), 1)
    ).astype(F32).astype(BF16)
    for s in range(2):
        part = dot(eye, lat_v[s * cap : (s + 1) * cap, :], NT)
        position = lax.broadcasted_iota(jnp.int32, part.shape, 1)
        part = jnp.where(position < count[s], part, 0.0).astype(BF16)
        for b in range(n_x):
            lat_all[b, tp, :, s * cap : (s + 1) * cap] = part[b * n_lat // n_x : (b + 1) * n_lat // n_x]
    pl.semaphore_wait(barrier, len(peers))

    def gather(block, half):
        pairs = [sems.take() for _ in range(8)]

        def start():
            ship(block(tp), block(tp), {"tp": y_up}, pairs[0])
            ship(block(tp), block(tp), {"tp": y_dn}, pairs[1])
            ship(block(tp), block(tp), {"tp": partner}, pairs[2])

        def forward():
            arrive(block(y_dn), pairs[0])
            ship(half(y_dn, 0), half(y_dn, 0), {"tp": y_up}, pairs[3])
            ship(block(y_dn), block(y_dn), {"tp": partner}, pairs[5])
            arrive(block(y_up), pairs[1])
            ship(half(y_up, 1), half(y_up, 1), {"tp": y_dn}, pairs[4])
            ship(block(y_up), block(y_up), {"tp": partner}, pairs[6])

        def forward_far():
            arrive(half(y_far, 0), pairs[3])
            arrive(half(y_far, 1), pairs[4])
            ship(block(y_far), block(y_far), {"tp": partner}, pairs[7])

        def finish():
            arrive(block(tp_of(y, oc)), pairs[2])
            arrive(block(tp_of(y - 1, oc)), pairs[5])
            arrive(block(tp_of(y + 1, oc)), pairs[6])
            arrive(block(tp_of(y + 2, oc)), pairs[7])

        return start, forward, forward_far, finish

    def ring_sum(value, block, far, near, size, me, up, dn, across, device):
        pairs = [sems.take() for _ in range(6)]

        def first():
            ship(block(across, 0), far(0), device(up), pairs[0])
            ship(block(across, 1), far(1), device(dn), pairs[1])
            ship(block(up, 1), near(0, 1), device(up), pairs[2])
            ship(block(dn, 0), near(1, 0), device(dn), pairs[3])

        def second():
            arrive(far(0), pairs[0])
            block(up, 0)[...] = (value(up, 0) + far(0)[...].astype(F32)).astype(BF16)
            ship(block(up, 0), near(0, 0), device(up), pairs[4])
            arrive(far(1), pairs[1])
            block(dn, 1)[...] = (value(dn, 1) + far(1)[...].astype(F32)).astype(BF16)
            ship(block(dn, 1), near(1, 1), device(dn), pairs[5])

        def total():
            arrive(near(0, 1), pairs[2])
            arrive(near(1, 0), pairs[3])
            arrive(near(0, 0), pairs[4])
            arrive(near(1, 1), pairs[5])
            return [
                value(me, k) + near(0, k)[...].astype(F32) + near(1, k)[...].astype(F32)
                for k in range(2)
            ]

        return first, second, total

    lat_gather = gather(
        lambda i: lat_all.at[:, i],
        lambda i, k: lat_all.at[pl.ds(k * n_x // 2, n_x // 2), i],
    )

    pair_pairs = [sems.take() for _ in range(NH)]

    def weights(h):
        return w_v[h].reshape(rows_h, columns)

    def other_slot(h):
        pair_s[h] = dot(weights(h), g_v[oc], NT)
        ship(pair_s.at[h], pair_r.at[h], {"tp": partner}, pair_pairs[h])

    def own_slot(h):
        part = dot(weights(h), g_v[c], NT)
        for j in range(n_y):
            lg_s[h, j] = part[:, j * blk : (j + 1) * blk]

    def pair_sum(h):
        arrive(pair_r.at[h], pair_pairs[h])
        for j in range(n_y):
            both = lg_s[h, j] + pair_r[h, :, j * blk : (j + 1) * blk]
            lg_s[h, j] = both
            lg_b[h, j] = both.astype(BF16)

    def row_half(k, rows):
        return pl.ds(k * rows // 2, rows // 2)

    def lg_ring(h):
        return ring_sum(
            lambda j, k: lg_s[h, j, row_half(k, rows_h)],
            lambda j, k: lg_b.at[h, j, row_half(k, rows_h)],
            lambda k: lg_far.at[h, k],
            lambda s, k: lg_near.at[h, s, k],
            rows_h, y, lax.rem(y + 1, n_y), lax.rem(y + n_y - 1, n_y), lax.rem(y + 2, n_y),
            lambda j: {"tp": j * 2 + c},
        )

    lg_rings = [lg_ring(h) for h in range(NH)]

    def lg_gather(h):
        def columns_of(i):
            start = pl.multiple_of(lax.rem(i, 2) * cap + (i // 2) * blk, blk)
            return pl.ds(start, blk)

        return gather(
            lambda i: lg_all.at[h, :, columns_of(i)],
            lambda i, k: lg_all.at[h, row_half(k, rows_h), columns_of(i)],
        )

    lg_gathers = [lg_gather(h) for h in range(NH)]
    live = jnp.where(c == 0, count[0], count[1]) > y * blk

    def lg_final(h):
        for k, part in enumerate(lg_rings[h][2]()):
            start = pl.multiple_of(c * cap + y * blk, blk)
            part = jnp.where(live, part, 0.0).astype(BF16)
            lg_all[h, row_half(k, rows_h), pl.ds(start, blk)] = part
        lg_gathers[h][0]()

    def up_ring(q):
        return ring_sum(
            lambda j, k: u_b[q, j, row_half(k, u_b.shape[2])].astype(F32),
            lambda j, k: u_b.at[q, j, row_half(k, u_b.shape[2])],
            lambda k: u_far.at[q, k],
            lambda s, k: u_near.at[q, s, k],
            u_b.shape[2], x, x_up, x_dn, x_far, lambda j: {"dp": j},
        )

    up_rings = [up_ring(q) for q in range(NU)]

    def up_part(q):
        lhs = lat_all[...].reshape(-1, 2 * cap)
        rhs = g_v[:, :, q * nq : (q + 1) * nq].reshape(2 * cap, nq)
        part = dot(lhs, rhs, NN)
        for b in range(n_x):
            u_b[q, b] = part[b * u_b.shape[2] : (b + 1) * u_b.shape[2]].astype(BF16)
        up_rings[q][0]()

    up_pairs = [[sems.take() for _ in z_peers] for _ in range(NU)]

    def up_scatter(q):
        halves = up_rings[q][2]()
        per_half = n_z // 2
        for k in range(2):
            zs_u[q, k * per_half : (k + 1) * per_half] = (
                halves[k].reshape(per_half, -1, nq).astype(BF16)
            )
        zr_u[q, z] = zs_u[q, z]
        for p, pair in zip(z_peers, up_pairs[q]):
            ship(zs_u.at[q, p], zr_u.at[q, z], {"mb": p}, pair)

    def up_total(q):
        for d, pair in enumerate(up_pairs[q]):
            arrive(zr_u.at[q, lax.rem(z + n_z - 1 - d, n_z)], pair)
        total = zr_u[q, 0].astype(F32)
        for p in range(1, n_z):
            total += zr_u[q, p].astype(F32)
        up_out[:, q * nq : (q + 1) * nq] = total

    def down_ring(h):
        return ring_sum(
            lambda j, k: d_s[h, j, row_half(k, rx)],
            lambda j, k: d_b.at[h, j, row_half(k, rx)],
            lambda k: d_far.at[h, k],
            lambda s, k: d_near.at[h, s, k],
            rx, x, x_up, x_dn, x_far, lambda j: {"dp": j},
        )

    down_rings = [down_ring(h) for h in range(NH)]

    def down_part(h):
        lhs = lg_all[h]
        for start in range(0, width, 256):
            stop = min(start + 256, width)
            part = dot(lhs, h_v[:, start:stop], NN)
            for j in range(n_x):
                rows = part[j * rx : (j + 1) * rx]
                d_s[h, j, :, start:stop] = rows
                d_b[h, j, :, start:stop] = rows.astype(BF16)
        down_rings[h][0]()

    out_pairs = [[sems.take() for _ in z_peers] for _ in range(NH)]
    back_pairs = [[sems.take() for _ in z_peers] for _ in range(NH)]

    def down_scatter(h):
        halves = down_rings[h][2]()
        per_half = n_z // 2
        for k in range(2):
            zs_d[h, k * per_half : (k + 1) * per_half] = (
                halves[k].reshape(per_half, -1, width).astype(BF16)
            )
        zr_d[h, z] = zs_d[h, z]
        for p, pair in zip(z_peers, out_pairs[h]):
            ship(zs_d.at[h, p], zr_d.at[h, z], {"mb": p}, pair)

    def down_prefix(h):
        for d, pair in enumerate(out_pairs[h]):
            arrive(zr_d.at[h, lax.rem(z + n_z - 1 - d, n_z)], pair)
        total = zr_d[h, 0].astype(F32)
        po_d[h, 0] = total.astype(BF16)
        for p in range(1, n_z):
            total += zr_d[h, p].astype(F32)
            po_d[h, p] = total.astype(BF16)
        rf_d[h, z] = po_d[h, z]
        for p, pair in zip(z_peers, back_pairs[h]):
            ship(po_d.at[h, p], rf_d.at[h, z], {"mb": p}, pair)

    def down_arrive(h):
        for d, pair in enumerate(back_pairs[h]):
            arrive(rf_d.at[h, lax.rem(z + n_z - 1 - d, n_z)], pair)

    lat_gather[0]()
    get_w[0].wait()
    get_g_other.wait()
    other_slot(0)
    get_g_own.wait()
    own_slot(0)
    for h in range(1, NH):
        get_w[h].wait()
        other_slot(h)
        pair_sum(h - 1)
        lg_rings[h - 1][0]()
        own_slot(h)
    pair_sum(NH - 1)
    lg_rings[NH - 1][0]()
    lat_gather[1]()
    for h in range(NH):
        lg_rings[h][1]()
    lat_gather[2]()
    lat_gather[3]()
    for h in range(NH):
        up_part(h)
        lg_final(h)
    up_part(2)
    lg_gathers[0][1]()
    up_part(3)
    lg_gathers[1][1]()
    up_rings[0][1]()
    lg_gathers[0][2]()
    lg_gathers[1][2]()
    get_h.wait()
    for h in range(NH):
        lg_gathers[h][3]()
        down_part(h)
    for q in range(1, NU):
        up_rings[q][1]()
    for h in range(NH):
        down_rings[h][1]()
    for q in range(NU):
        up_scatter(q)
    for h in range(NH):
        down_scatter(h)
    for h in range(NH):
        down_prefix(h)
    for q in range(NU):
        up_total(q)
    for h in range(NH):
        down_arrive(h)
    final = rf_d[...].astype(F32).reshape(NH * rx, width)
    down_out[...] = final.T
    for copy in sent:
        copy.wait_send()


def local(sizes, hidden, latent, out_grad, up_weight, mb_tokens, slot_mb):
    n_z, n_y, n_x = sizes
    slot_count, cap, width = hidden.shape[1:]
    rank, columns = up_weight.shape
    n_lat = latent.shape[3]
    row_total = slot_count * cap
    rows_h = rank // NH
    rx = rows_h // n_x
    blk = cap // n_y
    rows_u = rank // n_x
    nq = columns // NU
    any_space = pl.BlockSpec(memory_space=pl.ANY)
    n_sems = 8 + NH + 6 * NH + 8 * NH + 6 * NU + (n_z - 1) * NU + 6 * NH + 2 * (n_z - 1) * NH
    up_grad, running = pl.pallas_call(
        functools.partial(kernel, n_z, n_y, n_x),
        out_shape=(
            jax.ShapeDtypeStruct((rows_u // n_z, columns), F32),
            jax.ShapeDtypeStruct((width, rank // n_x), F32),
        ),
        in_specs=[any_space] * 4 + [pl.BlockSpec(memory_space=pltpu.SMEM)] * 2,
        out_specs=(pl.BlockSpec(memory_space=pltpu.VMEM),) * 2,
        scratch_shapes=[
            pltpu.VMEM((row_total, n_lat), BF16),
            pltpu.VMEM((row_total, width), BF16),
            pltpu.VMEM((slot_count, cap, columns), BF16),
            pltpu.VMEM((NH, n_x, rx, columns), BF16),
            pltpu.VMEM((n_x, 2 * n_y, n_lat // n_x, row_total), BF16),
            pltpu.VMEM((NH, rows_h, cap), F32),
            pltpu.VMEM((NH, rows_h, cap), F32),
            pltpu.VMEM((NH, n_y, rows_h, blk), F32),
            pltpu.VMEM((NH, n_y, rows_h, blk), BF16),
            pltpu.VMEM((NH, 2, rows_h // 2, blk), BF16),
            pltpu.VMEM((NH, 2, 2, rows_h // 2, blk), BF16),
            pltpu.VMEM((NH, rows_h, row_total), BF16),
            pltpu.VMEM((NH, n_x, rx, width), F32),
            pltpu.VMEM((NH, n_x, rx, width), BF16),
            pltpu.VMEM((NH, 2, rx // 2, width), BF16),
            pltpu.VMEM((NH, 2, 2, rx // 2, width), BF16),
            pltpu.VMEM((NH, n_z, rx // n_z, width), BF16),
            pltpu.VMEM((NH, n_z, rx // n_z, width), BF16),
            pltpu.VMEM((NH, n_z, rx // n_z, width), BF16),
            pltpu.VMEM((NH, n_z, rx // n_z, width), BF16),
            pltpu.VMEM((NU, n_x, rows_u, nq), BF16),
            pltpu.VMEM((NU, 2, rows_u // 2, nq), BF16),
            pltpu.VMEM((NU, 2, 2, rows_u // 2, nq), BF16),
            pltpu.VMEM((NU, n_z, rows_u // n_z, nq), BF16),
            pltpu.VMEM((NU, n_z, rows_u // n_z, nq), BF16),
            pltpu.SemaphoreType.DMA((8,)),
            pltpu.SemaphoreType.DMA((n_sems,)),
            pltpu.SemaphoreType.DMA((n_sems,)),
        ],
        compiler_params=pltpu.CompilerParams(
            collective_id=0, has_side_effects=True, vmem_limit_bytes=62 * 1024 * 1024
        ),
    )(
        hidden.reshape(row_total, width),
        latent.reshape(row_total, n_lat),
        out_grad.reshape(slot_count, cap, columns),
        up_weight.reshape(n_x, NH, rx, columns),
        mb_tokens,
        slot_mb,
    )
    return up_grad, running[None]


def solution(mesh):
    sizes = (mesh.shape["mb"], mesh.shape["tp"] // 2, mesh.shape["dp"])
    return jax.shard_map(
        functools.partial(local, sizes),
        mesh=mesh,
        in_specs=(
            P("dp", "mb", None, "tp"),
            P("dp", "mb", None, "tp"),
            P("dp", "mb", None, "tp"),
            P(None, "tp"),
            P("dp", None),
            P("dp", "mb"),
        ),
        out_specs=(P(("mb", "dp"), "tp"), P("mb", "tp", "dp")),
        check_vma=False,
    )
```

time: 199 us -> 75.3 us (0.38)
  waiting for transfers between devices: 107 us -> 0 us
  Pallas kernels: 0 us -> 68.8 us
  blocking collectives: 27.2 us -> 0 us
  between operations: 15.6 us -> 0.64 us
  matrix products: 14.4 us -> 0 us
  starting transfers between devices: 13.3 us -> 0 us
  other arithmetic: 11.2 us -> 0 us
  local copies, waits for them, and re-layouts: 9.61 us -> 5.13 us
    pallas_call x0 -> x1, Pallas kernels: none -> 68.8 us  [local(): pl.pallas_call(functools.partial(kernel, n_z, n_y, n_x), out_shape=(jax.S...]
    reduce_scatter x2 -> x0, waiting for transfers between devices: 59.1 us -> none  [the longest x1 34.3 us: total_of(): own = lax.psum_scatter(padded, axis, scatter_dimension=0, tiled=True)]
    all_to_all x1 -> x0, blocking collectives: 27.2 us -> none  [summed_on_arrival(): lax.all_to_all(blocks, axis, split_axis=0, concat_axis=0, tiled=True)]
    all_gather x2 -> x0, waiting for transfers between devices: 26.9 us -> none  [the longest x1 26.9 us: local(): shard_rows = lax.all_gather(down_share[None], 'mb', axis=0, tiled=True)]
    all_to_all x2 -> x0, waiting for transfers between devices: 21.4 us -> none  [the longest x1 12.1 us: copy_for_each(): return lax.all_to_all(copies, axis, split_axis=0, concat_axis=0, tiled=True)]
    dot_general x4 -> x0, matrix products: 14.4 us -> none  [the longest x1 6.63 us: local(): lax.dot_general(factors, masked_grads, (((0,), (0,)), ((), ())), preferre...]
    all_to_all x2 -> x0, starting transfers between devices: 13.2 us -> none  [the longest x1 8.94 us: copy_for_each(): return lax.all_to_all(copies, axis, split_axis=0, concat_axis=0, tiled=True)]
    select_n x2 -> x0, other arithmetic: 7.03 us -> none  [local(): jnp.where(valid_rows[:, :, None], out_grad[0], jnp.zeros((), out_grad.dty...]
  transfers between devices with their start and end apart: 6 -> 0, of which waited for: 5 -> 0; matrix products, arithmetic and copies ran while one was open for 12% -> 0% of each run, Pallas kernels for 0% -> 0%
where the time goes in v1:
time: 75.3 us; the launch traced here: 74.6 us
  Pallas kernels  68.8 us (91%)
  local copies, waits for them, and re-layouts  5.13 us (7%)
    pallas_call x1, Pallas kernels, local(): pl.pallas_call(functools.partial(kernel, n_z, n_y, n_x), out_shape=(jax.S...  68.8 us
    unnamed x3, local copies, waits for them, and re-layouts  5.13 us

profile of v1, /device:TPU:16, one launch (start us, length us, event | category | flops | bytes accessed | tf_op | source)
XLA Modules:
  0.0 74.6 jit_solution(4685523729695830790)
XLA Ops:
  0.6 1.7 %copy.8 = bf16[1,2,512,64]{3,2,1,0:T(8,128)(2,1)} copy(bf16[1,2,512,64]{2,3,1,0:T(8,128)(2,1)} %param.7) | data formatting | bytes 262144 | tf_op args[1]
  2.4 68.8 %shard_map.77 = (f32[16,2048]{1,0:T(8,128)}, f32[896,128]{1,0:T(8,128)}) custom-call(bf16[1024,896]{1,0:T(8,128)(2,1)} %bitcast.7, bf16[1024,64]{1,0:T(8,128)(2,1)} %bitcast.8, bf16[2,512,2048]{2,1,0:T(8,128)(2,1)} %bitcast.5, bf16[4,2,64,2048]{3,2,1,0:T(8,128)(2,1)} %bitcast.6, s32[1,16]{1,0:T(1,128)} %tokens.1, s32[1,2]{1,0:T(1,128)} %slots.1), custom_call_target="tpu_custom_call" | custom-call | tf_op jit(solution)/shard_map/pallas_call | solution.py:394
  71.2 1.6 %copy.11 = f32[16,2048]{1,0:T(8,128)} copy(f32[16,2048]{1,0:T(8,128)} %get-tuple-element.8) | data formatting | bytes 262144
  72.7 1.8 %copy.12 = f32[1,896,128]{2,1,0:T(8,128)} copy(f32[1,896,128]{2,1,0:T(8,128)} %bitcast.9) | data formatting | bytes 917504

commit v2 on v1

v2 whole, which is shorter than its diff:
```python
import collections
import functools

import jax
import jax.numpy as jnp
from jax import lax
from jax.experimental import pallas as pl
from jax.experimental.pallas import tpu as pltpu
from jax.sharding import PartitionSpec as P

MESH = pl.DeviceIdType.MESH
F32 = jnp.float32
BF16 = jnp.bfloat16
NT = (((1,), (1,)), ((), ()))
NN = (((1,), (0,)), ((), ()))
NH = 2
NG = 4


def dot(a, b, dims):
    return lax.dot_general(a, b, dims, preferred_element_type=F32)


Gather = collections.namedtuple(
    "Gather", ["near", "across", "along", "across_halves", "far", "across_far", "finish"]
)
Ring = collections.namedtuple("Ring", ["far", "near", "second", "total"])


class Sems:
    def __init__(self, send, recv):
        self.send, self.recv, self.used = send, recv, 0

    def take(self):
        at = self.used
        self.used += 1
        return self.send.at[at], self.recv.at[at]


def kernel(
    n_z, n_y, n_x,
    hidden, latent, out_grad, weight, tokens_in, slots_in,
    up_out, down_out,
    tokens, slots,
    lat_v, h_v, g_v, w_v, lat_all,
    pair_s, pair_r, lg_s, lg_b, lg_in, lg_all,
    d_s, d_b, d_far, d_near, zs_d, zr_d, po_d, rf_d,
    u_b, u_far, u_near, t_u, t_pair, f_u, zr_u,
    load, send, recv,
):
    z = lax.axis_index("mb")
    tp = lax.axis_index("tp")
    x = lax.axis_index("dp")
    y, c = tp // 2, tp % 2
    oc = 1 - c
    cap = g_v.shape[1]
    blk = cap // n_y
    rows_h = lg_all.shape[1]
    rx = rows_h // n_x
    width = h_v.shape[1]
    columns = g_v.shape[2]
    half_c = columns // 2
    split = (width // 2 + 127) // 128 * 128

    def tp_of(row, core):
        return lax.rem(row + 2 * n_y, n_y) * 2 + core

    y_up, y_dn, y_far = tp_of(y + 1, c), tp_of(y - 1, c), tp_of(y + 2, c)
    x_up, x_dn, x_far = lax.rem(x + 1, n_x), lax.rem(x + n_x - 1, n_x), lax.rem(x + 2, n_x)
    partner = tp_of(y, oc)
    peers = [{"tp": partner}, {"tp": y_up}, {"tp": y_dn}]
    peers += [{"tp": y_far}]
    peers += [{"dp": x_up}, {"dp": x_dn}]
    hops = sorted(range(1, n_z), key=lambda d: -min(d, n_z - d))
    z_peers = [lax.rem(z + d, n_z) for d in hops]
    z_sources = [lax.rem(z + n_z - d, n_z) for d in hops]
    peers += [{"mb": p} for p in z_peers]

    loads = []

    def fetch(src, dst):
        copy = pltpu.make_async_copy(src, dst, load.at[len(loads)])
        copy.start()
        loads.append(copy)
        return copy

    barrier = pltpu.get_barrier_semaphore()
    for peer in peers:
        pl.semaphore_signal(barrier, inc=1, device_id=peer, device_id_type=MESH)
    get_lat = fetch(latent, lat_v)
    get_scalars = [fetch(tokens_in, tokens), fetch(slots_in, slots)]
    get_w = [fetch(weight.at[:, 0], w_v.at[0])]
    get_g_other = fetch(out_grad.at[oc], g_v.at[oc])
    get_g_own = fetch(out_grad.at[c], g_v.at[c])
    get_w += [fetch(weight.at[:, h], w_v.at[h]) for h in range(1, NH)]
    get_h = fetch(hidden, h_v)

    sent = []
    sems = Sems(send, recv)

    def ship(src, dst, device, pair):
        copy = pltpu.make_async_remote_copy(
            src_ref=src, dst_ref=dst, send_sem=pair[0], recv_sem=pair[1],
            device_id=device, device_id_type=MESH,
        )
        copy.start()
        sent.append(copy)

    def arrive(dst, pair):
        pltpu.make_async_remote_copy(
            src_ref=dst, dst_ref=dst, send_sem=pair[0], recv_sem=pair[1],
            device_id={"tp": partner}, device_id_type=MESH,
        ).wait_recv()

    for copy in get_scalars:
        copy.wait()
    count = [tokens[0, slots[0, s]] for s in range(2)]

    get_lat.wait()
    n_lat = lat_v.shape[1]
    for s in range(2):
        part = lat_v[s].astype(F32)
        position = lax.broadcasted_iota(jnp.int32, part.shape, 1)
        part = jnp.where(position < count[s], part, 0.0).astype(BF16)
        lat_all[tp, :, s * cap : (s + 1) * cap] = part
    pl.semaphore_wait(barrier, len(peers))

    def row_half(k, rows):
        return pl.ds(k * rows // 2, rows // 2)

    def gather(block, half):
        pairs = [sems.take() for _ in range(8)]

        def near():
            ship(block(tp), block(tp), {"tp": y_up}, pairs[0])
            ship(block(tp), block(tp), {"tp": y_dn}, pairs[1])
            ship(block(tp), block(tp), {"tp": partner}, pairs[2])

        def across():
            arrive(block(y_dn), pairs[0])
            ship(block(y_dn), block(y_dn), {"tp": partner}, pairs[5])
            arrive(block(y_up), pairs[1])
            ship(block(y_up), block(y_up), {"tp": partner}, pairs[6])

        def along():
            ship(half(y_dn, 0), half(y_dn, 0), {"tp": y_up}, pairs[3])
            ship(half(y_up, 1), half(y_up, 1), {"tp": y_dn}, pairs[4])

        def across_halves():
            arrive(half(y_far, 0), pairs[3])
            arrive(half(y_far, 1), pairs[4])
            ship(block(y_far), block(y_far), {"tp": partner}, pairs[7])

        def far():
            ship(block(tp), block(tp), {"tp": y_far}, pairs[3])

        def across_far():
            arrive(block(y_far), pairs[3])
            ship(block(y_far), block(y_far), {"tp": partner}, pairs[7])

        def finish(*which):
            for k in which:
                arrive(block(tp_of(y + (0, -1, 1, 2)[k], oc)), pairs[(2, 5, 6, 7)[k]])

        return Gather(near, across, along, across_halves, far, across_far, finish)

    def ring_sum(value, block, far, near, me, up, dn, across, device):
        pairs = [sems.take() for _ in range(6)]

        def send_far():
            ship(block(across, 0), far(0), device(up), pairs[0])
            ship(block(across, 1), far(1), device(dn), pairs[1])

        def send_near():
            ship(block(up, 1), near(0, 1), device(up), pairs[2])
            ship(block(dn, 0), near(1, 0), device(dn), pairs[3])

        def second():
            arrive(far(0), pairs[0])
            block(up, 0)[...] = (value(up, 0) + far(0)[...].astype(F32)).astype(BF16)
            ship(block(up, 0), near(0, 0), device(up), pairs[4])
            arrive(far(1), pairs[1])
            block(dn, 1)[...] = (value(dn, 1) + far(1)[...].astype(F32)).astype(BF16)
            ship(block(dn, 1), near(1, 1), device(dn), pairs[5])

        def total():
            arrive(near(0, 1), pairs[2])
            arrive(near(1, 0), pairs[3])
            arrive(near(0, 0), pairs[4])
            arrive(near(1, 1), pairs[5])
            return [
                value(me, k) + near(0, k)[...].astype(F32) + near(1, k)[...].astype(F32)
                for k in range(2)
            ]

        return Ring(send_far, send_near, second, total)

    lat_gather = gather(
        lambda i: lat_all.at[i],
        lambda i, k: lat_all.at[i, row_half(k, n_lat)],
    )

    pair_pairs = [sems.take() for _ in range(NH)]

    def weights(h):
        return w_v[h].reshape(rows_h, columns)

    def other_slot(h):
        pair_s[h] = dot(weights(h), g_v[oc], NT)
        ship(pair_s.at[h], pair_r.at[h], {"tp": partner}, pair_pairs[h])

    def own_slot(h):
        part = dot(weights(h), g_v[c], NT)
        for j in range(n_y):
            lg_s[h, j] = part[:, j * blk : (j + 1) * blk]

    def pair_sum(h):
        arrive(pair_r.at[h], pair_pairs[h])
        for j in range(n_y):
            both = lg_s[h, j] + pair_r[h, :, j * blk : (j + 1) * blk]
            lg_s[h, j] = both
            lg_b[h, j] = both.astype(BF16)

    lg_hops = (2, 1, n_y - 1)
    lg_pairs = [[sems.take() for _ in lg_hops] for _ in range(NH)]

    def lg_spread(h):
        for k, hop in enumerate(lg_hops):
            row = lax.rem(y + hop, n_y)
            ship(lg_b.at[h, row], lg_in.at[h, k], {"tp": row * 2 + c}, lg_pairs[h][k])

    def lg_gather(h):
        def columns_of(i):
            start = pl.multiple_of(lax.rem(i, 2) * cap + (i // 2) * blk, blk)
            return pl.ds(start, blk)

        return gather(
            lambda i: lg_all.at[h, :, columns_of(i)],
            lambda i, k: lg_all.at[h, row_half(k, rows_h), columns_of(i)],
        )

    lg_gathers = [lg_gather(h) for h in range(NH)]
    live = jnp.where(c == 0, count[0], count[1]) > y * blk

    def lg_final(h):
        total = lg_s[h, y]
        for k in range(len(lg_hops)):
            arrive(lg_in.at[h, k], lg_pairs[h][k])
            total += lg_in[h, k].astype(F32)
        start = pl.multiple_of(c * cap + y * blk, blk)
        lg_all[h, :, pl.ds(start, blk)] = jnp.where(live, total, 0.0).astype(BF16)
        lg_gathers[h].far()
        lg_gathers[h].near()

    rows_of = [lax.rem(y + n_y + off, n_y) for off in (0, 1, -1, 2)]
    parity = lax.rem(z, 2)
    across_z = [lax.rem(z + n_z + 1 - 2 * lax.rem(z + k, 2), n_z) for k in range(2)]
    swap_pairs = [[sems.take() for _ in range(2)] for _ in range(NG)]

    def column_half(k):
        return pl.ds(k * half_c, half_c)

    def up_ring(g):
        return ring_sum(
            lambda j, k: u_b[g, j, :, :, column_half(k)].astype(F32),
            lambda j, k: u_b.at[g, j, :, :, column_half(k)],
            lambda k: u_far.at[g, k],
            lambda s, k: u_near.at[g, s, k],
            x, x_up, x_dn, x_far, lambda j: {"dp": j},
        )

    up_rings = [up_ring(g) for g in range(NG)]

    def up_part(g):
        rows = n_lat // n_x
        lhs = lat_all[pl.ds(rows_of[g] * 2, 2)].reshape(2 * n_lat, 2 * cap)
        step = 512
        for start in range(0, columns, step):
            rhs = g_v[:, :, start : start + step].reshape(2 * cap, step)
            part = dot(lhs, rhs, NN).astype(BF16)
            for k in range(2):
                for b in range(n_x):
                    at = k * n_lat + b * rows
                    u_b[g, b, k, :, start : start + step] = part[at : at + rows]

    def up_total(g):
        for k, part in enumerate(up_rings[g].total()):
            t_u[g, :, :, column_half(k)] = part.astype(BF16)
        for k in range(2):
            ship(
                t_u.at[g, 1 - parity, :, column_half(k)], t_pair.at[g, k],
                {"mb": across_z[k]}, swap_pairs[g][k],
            )

    up_hops = range(2, n_z, 2)
    up_base = sems.used
    up_pairs = [sems.take() for _ in up_hops]
    to_owner = []

    def up_owner(g):
        for k in range(2):
            arrive(t_pair.at[g, k], swap_pairs[g][k])
            both = t_u[g, parity, :, column_half(k)].astype(F32) + t_pair[g, k].astype(F32)
            f_u[rows_of[g], :, column_half(k)] = both.astype(BF16)
        owner = 2 * rows_of[g] + parity
        hop = lax.rem(owner - z + n_z, n_z) // 2
        at = lax.rem(hop + n_z // 2 - 1, n_z // 2)
        slot = jnp.minimum(at, n_z // 2 - 2)
        copy = pltpu.make_async_remote_copy(
            src_ref=f_u.at[rows_of[g]], dst_ref=zr_u.at[slot],
            send_sem=send.at[up_base + slot], recv_sem=recv.at[up_base + slot],
            device_id={"mb": owner}, device_id_type=MESH,
        )
        pl.when(owner != z)(copy.start)
        to_owner.append((owner, copy))

    def up_final():
        total = f_u[z // 2].astype(F32)
        for d, pair in enumerate(up_pairs):
            arrive(zr_u.at[d], pair)
            total += zr_u[d].astype(F32)
        up_out[...] = total

    cuts = [(h, lo, hi) for h in range(NH) for lo, hi in ((0, split), (split, width))]

    def down_ring(h, lo, hi):
        return ring_sum(
            lambda j, k: d_s[h, j, row_half(k, rx), lo:hi],
            lambda j, k: d_b.at[h, j, row_half(k, rx), lo:hi],
            lambda k: d_far.at[h, k, :, lo:hi],
            lambda s, k: d_near.at[h, s, k, :, lo:hi],
            x, x_up, x_dn, x_far, lambda j: {"dp": j},
        )

    down_rings = [down_ring(*cut) for cut in cuts]

    def down_part(i):
        h, lo, hi = cuts[i]
        lhs = lg_all[h]
        for start in range(lo, hi, 256):
            stop = min(start + 256, hi)
            part = dot(lhs, h_v[:, start:stop], NN)
            for j in range(n_x):
                rows = part[j * rx : (j + 1) * rx]
                d_s[h, j, :, start:stop] = rows
                d_b[h, j, :, start:stop] = rows.astype(BF16)

    out_pairs = [[sems.take() for _ in z_peers] for _ in cuts]
    back_pairs = [[sems.take() for _ in z_peers] for _ in cuts]

    def down_scatter(i):
        h, lo, hi = cuts[i]
        halves = down_rings[i].total()
        per_half = n_z // 2
        for k in range(2):
            zs_d[h, k * per_half : (k + 1) * per_half, :, lo:hi] = (
                halves[k].reshape(per_half, -1, hi - lo).astype(BF16)
            )
        zr_d[h, z, :, lo:hi] = zs_d[h, z, :, lo:hi]
        for p, pair in zip(z_peers, out_pairs[i]):
            ship(zs_d.at[h, p, :, lo:hi], zr_d.at[h, z, :, lo:hi], {"mb": p}, pair)

    def down_prefix(i):
        h, lo, hi = cuts[i]
        for p, pair in zip(z_sources, out_pairs[i]):
            arrive(zr_d.at[h, p, :, lo:hi], pair)
        total = zr_d[h, 0, :, lo:hi].astype(F32)
        po_d[h, 0, :, lo:hi] = total.astype(BF16)
        for p in range(1, n_z):
            total += zr_d[h, p, :, lo:hi].astype(F32)
            po_d[h, p, :, lo:hi] = total.astype(BF16)
        rf_d[h, z, :, lo:hi] = po_d[h, z, :, lo:hi]
        for p, pair in zip(z_peers, back_pairs[i]):
            ship(po_d.at[h, p, :, lo:hi], rf_d.at[h, z, :, lo:hi], {"mb": p}, pair)

    def down_arrive(i):
        h, lo, hi = cuts[i]
        for p, pair in zip(z_sources, back_pairs[i]):
            arrive(rf_d.at[h, p, :, lo:hi], pair)

    lat_gather.near()
    get_w[0].wait()
    get_g_other.wait()
    other_slot(0)
    get_g_own.wait()
    own_slot(0)
    get_w[1].wait()
    other_slot(1)
    pair_sum(0)
    lg_spread(0)
    own_slot(1)
    pair_sum(1)
    lg_spread(1)
    lat_gather.finish(0)
    up_part(0)
    up_rings[0].far()
    up_rings[0].near()
    lat_gather.across()
    lat_gather.finish(2)
    up_part(1)
    up_rings[1].far()
    lat_gather.finish(1)
    up_part(2)
    up_rings[0].second()
    up_rings[1].near()
    lg_final(0)
    up_rings[2].far()
    lg_final(1)
    lat_gather.along()
    up_rings[1].second()
    up_rings[2].near()
    up_total(0)
    lg_gathers[0].across_far()
    lg_gathers[0].across()
    up_rings[2].second()
    get_h.wait()
    lg_gathers[0].finish(0, 1, 2, 3)
    down_part(0)
    down_rings[0].far()
    down_part(1)
    down_rings[1].far()
    down_rings[0].near()
    down_rings[1].near()
    lg_gathers[1].across_far()
    up_total(1)
    lg_gathers[1].across()
    lg_gathers[1].finish(0, 1, 2, 3)
    down_part(2)
    down_rings[2].far()
    down_part(3)
    down_rings[3].far()
    up_total(2)
    lat_gather.across_halves()
    down_rings[0].second()
    down_rings[1].second()
    down_rings[2].near()
    down_rings[3].near()
    up_owner(0)
    up_owner(1)
    lat_gather.finish(3)
    up_part(3)
    up_owner(2)
    down_rings[2].second()
    down_rings[3].second()
    up_rings[3].far()
    up_rings[3].near()
    down_scatter(0)
    down_scatter(1)
    down_scatter(2)
    down_scatter(3)
    up_rings[3].second()
    down_prefix(0)
    down_prefix(1)
    up_total(3)
    down_prefix(2)
    down_prefix(3)
    up_owner(3)
    down_arrive(0)
    down_arrive(1)
    down_arrive(2)
    down_arrive(3)
    up_final()
    down_out[...] = rf_d[...].astype(F32).reshape(NH * rx, width).astype(BF16)
    for copy in sent:
        copy.wait_send()
    for owner, copy in to_owner:
        pl.when(owner != z)(copy.wait_send)


def finish_kernel(up_in, down_in, up_out, down_out):
    up_out[...] = up_in[...]
    down_out[...] = down_in[...].astype(F32).T


def local(sizes, hidden, latent, out_grad, up_weight, mb_tokens, slot_mb):
    n_z, n_y, n_x = sizes
    slot_count, cap, width = hidden.shape[1:]
    rank, columns = up_weight.shape
    n_lat = latent.shape[3]
    row_total = slot_count * cap
    rows_h = rank // NH
    rx = rows_h // n_x
    blk = cap // n_y
    rows_u = rank // n_x // n_z
    in_hbm = pl.BlockSpec(memory_space=pltpu.HBM)
    n_sems = 8 + NH + 3 * NH + 8 * NH + 8 * NG + (n_z // 2 - 1) + 2 * (6 + 2 * (n_z - 1)) * NH
    up_grad, running = pl.pallas_call(
        functools.partial(kernel, n_z, n_y, n_x),
        out_shape=(
            jax.ShapeDtypeStruct((rows_u, columns), F32),
            jax.ShapeDtypeStruct((rank // n_x, width), BF16),
        ),
        in_specs=[in_hbm] * 6,
        out_specs=(pl.BlockSpec(memory_space=pltpu.VMEM),) * 2,
        scratch_shapes=[
            pltpu.SMEM(mb_tokens.shape, jnp.int32),
            pltpu.SMEM(slot_mb.shape, jnp.int32),
            pltpu.VMEM((slot_count, n_lat, cap), BF16),
            pltpu.VMEM((row_total, width), BF16),
            pltpu.VMEM((slot_count, cap, columns), BF16),
            pltpu.VMEM((NH, n_x, rx, columns), BF16),
            pltpu.VMEM((2 * n_y, n_lat, row_total), BF16),
            pltpu.VMEM((NH, rows_h, cap), F32),
            pltpu.VMEM((NH, rows_h, cap), F32),
            pltpu.VMEM((NH, n_y, rows_h, blk), F32),
            pltpu.VMEM((NH, n_y, rows_h, blk), BF16),
            pltpu.VMEM((NH, 3, rows_h, blk), BF16),
            pltpu.VMEM((NH, rows_h, row_total), BF16),
            pltpu.VMEM((NH, n_x, rx, width), F32),
            pltpu.VMEM((NH, n_x, rx, width), BF16),
            pltpu.VMEM((NH, 2, rx // 2, width), BF16),
            pltpu.VMEM((NH, 2, 2, rx // 2, width), BF16),
            pltpu.VMEM((NH, n_z, rx // n_z, width), BF16),
            pltpu.VMEM((NH, n_z, rx // n_z, width), BF16),
            pltpu.VMEM((NH, n_z, rx // n_z, width), BF16),
            pltpu.VMEM((NH, n_z, rx // n_z, width), BF16),
            pltpu.VMEM((NG, n_x, 2, rows_u, columns), BF16),
            pltpu.VMEM((NG, 2, 2, rows_u, columns // 2), BF16),
            pltpu.VMEM((NG, 2, 2, 2, rows_u, columns // 2), BF16),
            pltpu.VMEM((NG, 2, rows_u, columns), BF16),
            pltpu.VMEM((NG, 2, rows_u, columns // 2), BF16),
            pltpu.VMEM((n_y, rows_u, columns), BF16),
            pltpu.VMEM((n_z // 2 - 1, rows_u, columns), BF16),
            pltpu.SemaphoreType.DMA((10,)),
            pltpu.SemaphoreType.DMA((n_sems,)),
            pltpu.SemaphoreType.DMA((n_sems,)),
        ],
        compiler_params=pltpu.CompilerParams(
            collective_id=0, has_side_effects=True, vmem_limit_bytes=66_400_000
        ),
    )(
        hidden.reshape(row_total, width),
        latent[0].swapaxes(1, 2),
        out_grad.reshape(slot_count, cap, columns),
        up_weight.reshape(n_x, NH, rx, columns),
        mb_tokens,
        slot_mb,
    )
    up_grad, running = pl.pallas_call(
        finish_kernel,
        out_shape=(
            jax.ShapeDtypeStruct((rows_u, columns), F32),
            jax.ShapeDtypeStruct((width, rank // n_x), F32),
        ),
        in_specs=[pl.BlockSpec(memory_space=pltpu.VMEM)] * 2,
        out_specs=(pl.BlockSpec(memory_space=pltpu.VMEM),) * 2,
        compiler_params=pltpu.CompilerParams(vmem_limit_bytes=8 * 1024 * 1024),
    )(up_grad, running)
    return up_grad, running[None]


def solution(mesh):
    sizes = (mesh.shape["mb"], mesh.shape["tp"] // 2, mesh.shape["dp"])
    return jax.shard_map(
        functools.partial(local, sizes),
        mesh=mesh,
        in_specs=(
            P("dp", "mb", None, "tp"),
            P("dp", "mb", None, "tp"),
            P("dp", "mb", None, "tp"),
            P(None, "tp"),
            P("dp", None),
            P("dp", "mb"),
        ),
        out_specs=(P(("mb", "dp"), "tp"), P("mb", "tp", "dp")),
        check_vma=False,
    )
```

time: 75.3 us -> 61.4 us (0.82)
  Pallas kernels: 68.8 us -> 58.8 us
  local copies, waits for them, and re-layouts: 5.13 us -> 1.84 us
    pallas_call x1, Pallas kernels: 68.8 us -> 57.9 us  [local(): pl.pallas_call(functools.partial(kernel, n_z, n_y, n_x), out_shape=(jax.S...]
    unnamed x3 -> x4, local copies, waits for them, and re-layouts: 5.13 us -> 1.84 us
    pallas_call x0 -> x1, Pallas kernels: none -> 0.9 us  [local(): pl.pallas_call(finish_kernel, out_shape=(jax.ShapeDtypeStruct((rows_u, co...]
where the time goes in v2:
time: 61.4 us; the launch traced here: 61.2 us
  Pallas kernels  58.8 us (96%)
  local copies, waits for them, and re-layouts  1.84 us (3%)
  between operations  0.65 us (1%)
    pallas_call x1, Pallas kernels, local(): pl.pallas_call(functools.partial(kernel, n_z, n_y, n_x), out_shape=(jax.S...  57.9 us
    unnamed x4, local copies, waits for them, and re-layouts  1.84 us

profile of v2, /device:TPU:16, one launch (start us, length us, event | category | flops | bytes accessed | tf_op | source)
XLA Modules:
  0.0 61.2 jit_solution(16868188312437621386)
XLA Ops:
  0.6 57.9 %shard_map.77 = (f32[16,2048]{1,0:T(8,128)}, bf16[128,896]{1,0:T(8,128)(2,1)}) custom-call(bf16[1024,896]{1,0:T(8,128)(2,1)} %bitcast.9, bf16[2,64,512]{2,1,0:T(8,128)(2,1)} %bitcast.10, bf16[2,512,2048]{2,1,0:T(8,128)(2,1)} %bitcast.7, bf16[4,2,64,2048]{3,2,1,0:T(8,128)(2,1)} %bitcast.8, s32[1,16]{1,0:T(1,128)} %tokens_in.1, s32[1,2]{1,0:T(1,128)} %slots_in.1), custom_call_target="tpu_custom_call" | custom-call | tf_op jit(solution)/shard_map/pallas_call | solution.py:487
  58.5 0.0 copy-start
  58.5 0.9 %copy-done = bf16[128,896]{1,0:T(8,128)(2,1)S(1)} copy-done((bf16[128,896]{1,0:T(8,128)(2,1)S(1)}, bf16[128,896]{1,0:T(8,128)(2,1)}, u32[]{:S(2)}) %copy-start) | copy-done | bytes 229400
  59.4 0.0 copy-start.1
  59.4 0.9 %copy-done.1 = f32[16,2048]{1,0:T(8,128)S(1)} copy-done((f32[16,2048]{1,0:T(8,128)S(1)}, f32[16,2048]{1,0:T(8,128)}, u32[]{:S(2)}) %copy-start.1) | copy-done | bytes 131096
  60.3 0.9 %shard_map.78 = (f32[16,2048]{1,0:T(8,128)}, f32[896,128]{1,0:T(8,128)}) custom-call(f32[16,2048]{1,0:T(8,128)S(1)} %copy-done.1, bf16[128,896]{1,0:T(8,128)(2,1)S(1)} %copy-done), custom_call_target="tpu_custom_call" | custom-call | tf_op jit(solution)/shard_map/pallas_call | solution.py:539
Async XLA Ops:
  58.5 0.9 %copy-start = (bf16[128,896]{1,0:T(8,128)(2,1)S(1)}, bf16[128,896]{1,0:T(8,128)(2,1)}, u32[]{:S(2)}) copy-start(bf16[128,896]{1,0:T(8,128)(2,1)} %get-tuple-element.7.down_in) | copy-start | bytes 688132
  59.4 0.9 %copy-start.1 = (f32[16,2048]{1,0:T(8,128)S(1)}, f32[16,2048]{1,0:T(8,128)}, u32[]{:S(2)}) copy-start(f32[16,2048]{1,0:T(8,128)} %get-tuple-element.6.up_in) | copy-start | bytes 393220

commit v3 on v2

--- a/solution.py
+++ b/solution.py
@@ -14,6 +14,7 @@
 NT = (((1,), (1,)), ((), ()))
 NN = (((1,), (0,)), ((), ()))
 NH = 2
+SWAPPED = 2
 NG = 4
 
 
@@ -40,13 +41,13 @@
 def kernel(
     n_z, n_y, n_x,
     hidden, latent, out_grad, weight, tokens_in, slots_in,
-    up_out, down_out,
+    zr_u, rf_d,
     tokens, slots,
     lat_v, h_v, g_v, w_v, lat_all,
     pair_s, pair_r, lg_s, lg_b, lg_in, lg_all,
-    d_s, d_b, d_far, d_near, zs_d, zr_d, po_d, rf_d,
-    u_b, u_far, u_near, t_u, t_pair, f_u, zr_u,
-    load, send, recv,
+    d_s, d_b, d_far, d_near, zs_d, zr_d, po_d,
+    u_b, u_pair, x_b, u_far, u_near, t_u, t_pair, f_u,
+    load, save, send, recv,
 ):
     z = lax.axis_index("mb")
     tp = lax.axis_index("tp")
@@ -96,7 +97,13 @@
     get_h = fetch(hidden, h_v)
 
     sent = []
+    kept = []
     sems = Sems(send, recv)
+
+    def keep(src, dst):
+        copy = pltpu.make_async_copy(src, dst, save.at[len(kept)])
+        copy.start()
+        kept.append(copy)
 
     def ship(src, dst, device, pair):
         copy = pltpu.make_async_remote_copy(
@@ -261,6 +268,14 @@
         return pl.ds(k * half_c, half_c)
 
     def up_ring(g):
+        if g == SWAPPED:
+            return ring_sum(
+                lambda j, k: x_b[j, :, column_half(k)].astype(F32),
+                lambda j, k: x_b.at[j, :, column_half(k)],
+                lambda k: u_far.at[g, k, 0],
+                lambda s, k: u_near.at[g, s, k, 0],
+                x, x_up, x_dn, x_far, lambda j: {"dp": j},
+            )
         return ring_sum(
             lambda j, k: u_b[g, j, :, :, column_half(k)].astype(F32),
             lambda j, k: u_b.at[g, j, :, :, column_half(k)],
@@ -282,6 +297,19 @@
                 for b in range(n_x):
                     at = k * n_lat + b * rows
                     u_b[g, b, k, :, start : start + step] = part[at : at + rows]
+            if g == SWAPPED and (start + step) % half_c == 0:
+                k = start // half_c
+                ship(
+                    u_b.at[g, :, 1 - parity, :, column_half(k)], u_pair.at[k],
+                    {"mb": across_z[k]}, swap_pairs[g][k],
+                )
+
+    def up_swap():
+        for k in range(2):
+            arrive(u_pair.at[k], swap_pairs[SWAPPED][k])
+            for b in range(n_x):
+                both = u_b[SWAPPED, b, parity, :, column_half(k)].astype(F32) + u_pair[k, b].astype(F32)
+                x_b[b, :, column_half(k)] = both.astype(BF16)
 
     def up_total(g):
         for k, part in enumerate(up_rings[g].total()):
@@ -298,7 +326,10 @@
     to_owner = []
 
     def up_owner(g):
-        for k in range(2):
+        if g == SWAPPED:
+            for k, part in enumerate(up_rings[g].total()):
+                f_u[rows_of[g], :, column_half(k)] = part.astype(BF16)
+        for k in range(2 if g != SWAPPED else 0):
             arrive(t_pair.at[g, k], swap_pairs[g][k])
             both = t_u[g, parity, :, column_half(k)].astype(F32) + t_pair[g, k].astype(F32)
             f_u[rows_of[g], :, column_half(k)] = both.astype(BF16)
@@ -312,14 +343,13 @@
             device_id={"mb": owner}, device_id_type=MESH,
         )
         pl.when(owner != z)(copy.start)
-        to_owner.append((owner, copy))
+        own = pltpu.make_async_copy(f_u.at[rows_of[g]], zr_u.at[n_z // 2 - 1], save.at[2 * NH + g])
+        pl.when(owner == z)(own.start)
+        to_owner.append((owner, copy, own))
 
     def up_final():
-        total = f_u[z // 2].astype(F32)
         for d, pair in enumerate(up_pairs):
             arrive(zr_u.at[d], pair)
-            total += zr_u[d].astype(F32)
-        up_out[...] = total
 
     cuts = [(h, lo, hi) for h in range(NH) for lo, hi in ((0, split), (split, width))]
 
@@ -369,7 +399,7 @@
         for p in range(1, n_z):
             total += zr_d[h, p, :, lo:hi].astype(F32)
             po_d[h, p, :, lo:hi] = total.astype(BF16)
-        rf_d[h, z, :, lo:hi] = po_d[h, z, :, lo:hi]
+        keep(po_d.at[h, z, :, lo:hi], rf_d.at[h, z, :, lo:hi])
         for p, pair in zip(z_peers, back_pairs[i]):
             ship(po_d.at[h, p, :, lo:hi], rf_d.at[h, z, :, lo:hi], {"mb": p}, pair)
 
@@ -388,13 +418,13 @@
     other_slot(1)
     pair_sum(0)
     lg_spread(0)
-    own_slot(1)
-    pair_sum(1)
-    lg_spread(1)
     lat_gather.finish(0)
     up_part(0)
     up_rings[0].far()
     up_rings[0].near()
+    own_slot(1)
+    pair_sum(1)
+    lg_spread(1)
     lat_gather.across()
     lat_gather.finish(2)
     up_part(1)
@@ -404,42 +434,42 @@
     up_rings[0].second()
     up_rings[1].near()
     lg_final(0)
-    up_rings[2].far()
     lg_final(1)
     lat_gather.along()
     up_rings[1].second()
-    up_rings[2].near()
     up_total(0)
     lg_gathers[0].across_far()
+    up_swap()
+    up_rings[2].far()
+    up_rings[2].near()
     lg_gathers[0].across()
-    up_rings[2].second()
+    up_total(1)
     get_h.wait()
     lg_gathers[0].finish(0, 1, 2, 3)
     down_part(0)
     down_rings[0].far()
     down_part(1)
     down_rings[1].far()
+    up_rings[2].second()
     down_rings[0].near()
     down_rings[1].near()
+    up_owner(0)
     lg_gathers[1].across_far()
-    up_total(1)
     lg_gathers[1].across()
     lg_gathers[1].finish(0, 1, 2, 3)
     down_part(2)
     down_rings[2].far()
     down_part(3)
     down_rings[3].far()
-    up_total(2)
-    lat_gather.across_halves()
+    up_owner(1)
     down_rings[0].second()
     down_rings[1].second()
     down_rings[2].near()
     down_rings[3].near()
-    up_owner(0)
-    up_owner(1)
+    up_owner(2)
+    lat_gather.across_halves()
     lat_gather.finish(3)
     up_part(3)
-    up_owner(2)
     down_rings[2].second()
     down_rings[3].second()
     up_rings[3].far()
@@ -460,16 +490,37 @@
     down_arrive(2)
     down_arrive(3)
     up_final()
-    down_out[...] = rf_d[...].astype(F32).reshape(NH * rx, width).astype(BF16)
     for copy in sent:
         copy.wait_send()
-    for owner, copy in to_owner:
+    for copy in kept:
+        copy.wait()
+    for owner, copy, own in to_owner:
         pl.when(owner != z)(copy.wait_send)
-
-
-def finish_kernel(up_in, down_in, up_out, down_out):
-    up_out[...] = up_in[...]
-    down_out[...] = down_in[...].astype(F32).T
+        pl.when(owner == z)(own.wait)
+
+
+def finish_kernel(up_in, down_in, up_out, down_out, up_v, down_v, up_w, down_w, load, save):
+    loads = [
+        pltpu.make_async_copy(src, dst, load.at[k])
+        for k, (src, dst) in enumerate(((down_in, down_v), (up_in, up_v)))
+    ]
+    saves = [
+        pltpu.make_async_copy(src, dst, save.at[k])
+        for k, (src, dst) in enumerate(((down_w, down_out), (up_w, up_out)))
+    ]
+    for copy in loads:
+        copy.start()
+    loads[0].wait()
+    down_w[...] = down_v[...].astype(F32).reshape(-1, down_v.shape[-1]).T
+    saves[0].start()
+    loads[1].wait()
+    total = up_v[0].astype(F32)
+    for k in range(1, up_v.shape[0]):
+        total += up_v[k].astype(F32)
+    up_w[...] = total
+    saves[1].start()
+    for copy in saves:
+        copy.wait()
 
 
 def local(sizes, hidden, latent, out_grad, up_weight, mb_tokens, slot_mb):
@@ -482,16 +533,18 @@
     rx = rows_h // n_x
     blk = cap // n_y
     rows_u = rank // n_x // n_z
+    up_shape = (n_z // 2, rows_u, columns)
+    down_shape = (NH, n_z, rx // n_z, width)
     in_hbm = pl.BlockSpec(memory_space=pltpu.HBM)
     n_sems = 8 + NH + 3 * NH + 8 * NH + 8 * NG + (n_z // 2 - 1) + 2 * (6 + 2 * (n_z - 1)) * NH
     up_grad, running = pl.pallas_call(
         functools.partial(kernel, n_z, n_y, n_x),
         out_shape=(
-            jax.ShapeDtypeStruct((rows_u, columns), F32),
-            jax.ShapeDtypeStruct((rank // n_x, width), BF16),
+            jax.ShapeDtypeStruct(up_shape, BF16),
+            jax.ShapeDtypeStruct(down_shape, BF16),
         ),
         in_specs=[in_hbm] * 6,
-        out_specs=(pl.BlockSpec(memory_space=pltpu.VMEM),) * 2,
+        out_specs=(in_hbm,) * 2,
         scratch_shapes=[
             pltpu.SMEM(mb_tokens.shape, jnp.int32),
             pltpu.SMEM(slot_mb.shape, jnp.int32),
@@ -510,18 +563,19 @@
             pltpu.VMEM((NH, n_x, rx, width), BF16),
             pltpu.VMEM((NH, 2, rx // 2, width), BF16),
             pltpu.VMEM((NH, 2, 2, rx // 2, width), BF16),
-            pltpu.VMEM((NH, n_z, rx // n_z, width), BF16),
-            pltpu.VMEM((NH, n_z, rx // n_z, width), BF16),
-            pltpu.VMEM((NH, n_z, rx // n_z, width), BF16),
-            pltpu.VMEM((NH, n_z, rx // n_z, width), BF16),
+            pltpu.VMEM(down_shape, BF16),
+            pltpu.VMEM(down_shape, BF16),
+            pltpu.VMEM(down_shape, BF16),
             pltpu.VMEM((NG, n_x, 2, rows_u, columns), BF16),
+            pltpu.VMEM((2, n_x, rows_u, columns // 2), BF16),
+            pltpu.VMEM((n_x, rows_u, columns), BF16),
             pltpu.VMEM((NG, 2, 2, rows_u, columns // 2), BF16),
             pltpu.VMEM((NG, 2, 2, 2, rows_u, columns // 2), BF16),
             pltpu.VMEM((NG, 2, rows_u, columns), BF16),
             pltpu.VMEM((NG, 2, rows_u, columns // 2), BF16),
             pltpu.VMEM((n_y, rows_u, columns), BF16),
-            pltpu.VMEM((n_z // 2 - 1, rows_u, columns), BF16),
             pltpu.SemaphoreType.DMA((10,)),
+            pltpu.SemaphoreType.DMA((2 * NH + NG,)),
             pltpu.SemaphoreType.DMA((n_sems,)),
             pltpu.SemaphoreType.DMA((n_sems,)),
         ],
@@ -542,9 +596,17 @@
             jax.ShapeDtypeStruct((rows_u, columns), F32),
             jax.ShapeDtypeStruct((width, rank // n_x), F32),
         ),
-        in_specs=[pl.BlockSpec(memory_space=pltpu.VMEM)] * 2,
-        out_specs=(pl.BlockSpec(memory_space=pltpu.VMEM),) * 2,
-        compiler_params=pltpu.CompilerParams(vmem_limit_bytes=8 * 1024 * 1024),
+        in_specs=[in_hbm] * 2,
+        out_specs=(in_hbm,) * 2,
+        scratch_shapes=[
+            pltpu.VMEM(up_shape, BF16),
+            pltpu.VMEM(down_shape, BF16),
+            pltpu.VMEM((rows_u, columns), F32),
+            pltpu.VMEM((width, rank // n_x), F32),
+            pltpu.SemaphoreType.DMA((2,)),
+            pltpu.SemaphoreType.DMA((2,)),
+        ],
+        compiler_params=pltpu.CompilerParams(vmem_limit_bytes=66_400_000),
     )(up_grad, running)
     return up_grad, running[None]
 

time: 61.4 us -> 56.3 us (0.917); the launches traced: 61.2 us -> 55.4 us
  Pallas kernels: 58.8 us -> 54.8 us
  local copies, waits for them, and re-layouts: 1.84 us -> 0 us
    pallas_call x1, Pallas kernels: 57.9 us -> 52.9 us  [local(): pl.pallas_call(functools.partial(kernel, n_z, n_y, n_x), out_shape=(jax.S...]
    unnamed x4 -> x0, local copies, waits for them, and re-layouts: 1.84 us -> none
    pallas_call x1, Pallas kernels: 0.9 us -> 1.92 us  [local(): pl.pallas_call(finish_kernel, out_shape=(jax.ShapeDtypeStruct((rows_u, co...]
where the time goes in v3:
time: 56.3 us; the launch traced here: 55.4 us
  Pallas kernels  54.8 us (97%)
  between operations  0.64 us (1%)
    pallas_call x1, Pallas kernels, local(): pl.pallas_call(functools.partial(kernel, n_z, n_y, n_x), out_shape=(jax.S...  52.9 us
    pallas_call x1, Pallas kernels, local(): pl.pallas_call(finish_kernel, out_shape=(jax.ShapeDtypeStruct((rows_u, co...  1.92 us

profile of v3, /device:TPU:16, one launch (start us, length us, event | category | flops | bytes accessed | tf_op | source)
XLA Modules:
  0.0 55.4 jit_solution(15942141261111770621)
XLA Ops:
  0.6 52.9 %shard_map.77 = (bf16[4,16,2048]{2,1,0:T(8,128)(2,1)}, bf16[2,8,8,896]{3,2,1,0:T(8,128)(2,1)}) custom-call(bf16[1024,896]{1,0:T(8,128)(2,1)} %bitcast.9, bf16[2,64,512]{2,1,0:T(8,128)(2,1)} %bitcast.10, bf16[2,512,2048]{2,1,0:T(8,128)(2,1)} %bitcast.7, bf16[4,2,64,2048]{3,2,1,0:T(8,128)(2,1)} %bitcast.8, s32[1,16]{1,0:T(1,128)} %tokens_in.1, s32[1,2]{1,0:T(1,128)} %slots_in.1), custom_call_target="tpu_custom_call" | custom-call | tf_op jit(solution)/shard_map/pallas_call | solution.py:540
  53.5 1.9 %shard_map.78 = (f32[16,2048]{1,0:T(8,128)}, f32[896,128]{1,0:T(8,128)}) custom-call(bf16[4,16,2048]{2,1,0:T(8,128)(2,1)} %get-tuple-element.6.up_in, bf16[2,8,8,896]{3,2,1,0:T(8,128)(2,1)} %get-tuple-element.7.down_in), custom_call_target="tpu_custom_call" | custom-call | tf_op jit(solution)/shard_map/pallas_call | solution.py:593

commit v4 on v3

--- a/solution.py
+++ b/solution.py
@@ -14,7 +14,7 @@
 NT = (((1,), (1,)), ((), ()))
 NN = (((1,), (0,)), ((), ()))
 NH = 2
-SWAPPED = 2
+SWAPPED = (2,)
 NG = 4
 
 
@@ -30,12 +30,14 @@
 
 class Sems:
     def __init__(self, send, recv):
-        self.send, self.recv, self.used = send, recv, 0
-
-    def take(self):
-        at = self.used
-        self.used += 1
-        return self.send.at[at], self.recv.at[at]
+        self.send, self.recv, self.used = send, recv, [0, 0]
+
+    def take(self, sends=1, recvs=1):
+        sends = self.send.at[self.used[0]] if sends else None
+        recvs = self.recv.at[self.used[1]] if recvs else None
+        self.used[0] += sends is not None
+        self.used[1] += recvs is not None
+        return sends, recvs
 
 
 def kernel(
@@ -74,7 +76,6 @@
     peers += [{"dp": x_up}, {"dp": x_dn}]
     hops = sorted(range(1, n_z), key=lambda d: -min(d, n_z - d))
     z_peers = [lax.rem(z + d, n_z) for d in hops]
-    z_sources = [lax.rem(z + n_z - d, n_z) for d in hops]
     peers += [{"mb": p} for p in z_peers]
 
     loads = []
@@ -105,17 +106,20 @@
         copy.start()
         kept.append(copy)
 
-    def ship(src, dst, device, pair):
+    drains = []
+
+    def ship(src, dst, device, pair, drain=True):
         copy = pltpu.make_async_remote_copy(
             src_ref=src, dst_ref=dst, send_sem=pair[0], recv_sem=pair[1],
             device_id=device, device_id_type=MESH,
         )
         copy.start()
-        sent.append(copy)
+        if drain:
+            sent.append(copy)
 
     def arrive(dst, pair):
         pltpu.make_async_remote_copy(
-            src_ref=dst, dst_ref=dst, send_sem=pair[0], recv_sem=pair[1],
+            src_ref=dst, dst_ref=dst, send_sem=send.at[0], recv_sem=pair[1],
             device_id={"tp": partner}, device_id_type=MESH,
         ).wait_recv()
 
@@ -171,30 +175,28 @@
 
         return Gather(near, across, along, across_halves, far, across_far, finish)
 
-    def ring_sum(value, block, far, near, me, up, dn, across, device):
-        pairs = [sems.take() for _ in range(6)]
+    def ring_sum(value, block, far, near, three, me, up, dn, across, device):
+        out, in_far, in_near = sems.take(1, 0), sems.take(0, 1), sems.take(0, 1)
+        to_far, to_near = (out[0], in_far[1]), (out[0], in_near[1])
+        drains.append((three, out))
 
         def send_far():
-            ship(block(across, 0), far(0), device(up), pairs[0])
-            ship(block(across, 1), far(1), device(dn), pairs[1])
+            ship(block(across, 0), far(0), device(up), to_far, False)
+            ship(block(across, 1), far(1), device(dn), to_far, False)
 
         def send_near():
-            ship(block(up, 1), near(0, 1), device(up), pairs[2])
-            ship(block(dn, 0), near(1, 0), device(dn), pairs[3])
+            ship(block(up, 1), near(0, 1), device(up), to_near, False)
+            ship(block(dn, 0), near(1, 0), device(dn), to_near, False)
 
         def second():
-            arrive(far(0), pairs[0])
+            arrive(far(None), in_far)
             block(up, 0)[...] = (value(up, 0) + far(0)[...].astype(F32)).astype(BF16)
-            ship(block(up, 0), near(0, 0), device(up), pairs[4])
-            arrive(far(1), pairs[1])
+            ship(block(up, 0), near(0, 0), device(up), to_near, False)
             block(dn, 1)[...] = (value(dn, 1) + far(1)[...].astype(F32)).astype(BF16)
-            ship(block(dn, 1), near(1, 1), device(dn), pairs[5])
+            ship(block(dn, 1), near(1, 1), device(dn), to_near, False)
 
         def total():
-            arrive(near(0, 1), pairs[2])
-            arrive(near(1, 0), pairs[3])
-            arrive(near(0, 0), pairs[4])
-            arrive(near(1, 1), pairs[5])
+            arrive(near(None, None), in_near)
             return [
                 value(me, k) + near(0, k)[...].astype(F32) + near(1, k)[...].astype(F32)
                 for k in range(2)
@@ -268,19 +270,22 @@
         return pl.ds(k * half_c, half_c)
 
     def up_ring(g):
-        if g == SWAPPED:
+        if g in SWAPPED:
+            at = SWAPPED.index(g)
             return ring_sum(
-                lambda j, k: x_b[j, :, column_half(k)].astype(F32),
-                lambda j, k: x_b.at[j, :, column_half(k)],
-                lambda k: u_far.at[g, k, 0],
-                lambda s, k: u_near.at[g, s, k, 0],
+                lambda j, k: x_b[at, j, :, column_half(k)].astype(F32),
+                lambda j, k: x_b.at[at, j, :, column_half(k)],
+                lambda k: u_far.at[g, :, 0] if k is None else u_far.at[g, k, 0],
+                lambda s, k: u_near.at[g, :, :, 0] if s is None else u_near.at[g, s, k, 0],
+                x_b.at[at, 0:3],
                 x, x_up, x_dn, x_far, lambda j: {"dp": j},
             )
         return ring_sum(
             lambda j, k: u_b[g, j, :, :, column_half(k)].astype(F32),
             lambda j, k: u_b.at[g, j, :, :, column_half(k)],
-            lambda k: u_far.at[g, k],
-            lambda s, k: u_near.at[g, s, k],
+            lambda k: u_far.at[g] if k is None else u_far.at[g, k],
+            lambda s, k: u_near.at[g] if s is None else u_near.at[g, s, k],
+            u_b.at[g, 0:3],
             x, x_up, x_dn, x_far, lambda j: {"dp": j},
         )
 
@@ -297,19 +302,20 @@
                 for b in range(n_x):
                     at = k * n_lat + b * rows
                     u_b[g, b, k, :, start : start + step] = part[at : at + rows]
-            if g == SWAPPED and (start + step) % half_c == 0:
+            if g in SWAPPED and (start + step) % half_c == 0:
                 k = start // half_c
                 ship(
-                    u_b.at[g, :, 1 - parity, :, column_half(k)], u_pair.at[k],
+                    u_b.at[g, :, 1 - parity, :, column_half(k)], u_pair.at[SWAPPED.index(g), k],
                     {"mb": across_z[k]}, swap_pairs[g][k],
                 )
 
-    def up_swap():
+    def up_swap(g):
+        at = SWAPPED.index(g)
         for k in range(2):
-            arrive(u_pair.at[k], swap_pairs[SWAPPED][k])
+            arrive(u_pair.at[at, k], swap_pairs[g][k])
             for b in range(n_x):
-                both = u_b[SWAPPED, b, parity, :, column_half(k)].astype(F32) + u_pair[k, b].astype(F32)
-                x_b[b, :, column_half(k)] = both.astype(BF16)
+                both = u_b[g, b, parity, :, column_half(k)].astype(F32) + u_pair[at, k, b].astype(F32)
+                x_b[at, b, :, column_half(k)] = both.astype(BF16)
 
     def up_total(g):
         for k, part in enumerate(up_rings[g].total()):
@@ -321,15 +327,15 @@
             )
 
     up_hops = range(2, n_z, 2)
-    up_base = sems.used
+    up_base = list(sems.used)
     up_pairs = [sems.take() for _ in up_hops]
     to_owner = []
 
     def up_owner(g):
-        if g == SWAPPED:
+        if g in SWAPPED:
             for k, part in enumerate(up_rings[g].total()):
                 f_u[rows_of[g], :, column_half(k)] = part.astype(BF16)
-        for k in range(2 if g != SWAPPED else 0):
+        for k in range(2 if g not in SWAPPED else 0):
             arrive(t_pair.at[g, k], swap_pairs[g][k])
             both = t_u[g, parity, :, column_half(k)].astype(F32) + t_pair[g, k].astype(F32)
             f_u[rows_of[g], :, column_half(k)] = both.astype(BF16)
@@ -339,7 +345,7 @@
         slot = jnp.minimum(at, n_z // 2 - 2)
         copy = pltpu.make_async_remote_copy(
             src_ref=f_u.at[rows_of[g]], dst_ref=zr_u.at[slot],
-            send_sem=send.at[up_base + slot], recv_sem=recv.at[up_base + slot],
+            send_sem=send.at[up_base[0] + slot], recv_sem=recv.at[up_base[1] + slot],
             device_id={"mb": owner}, device_id_type=MESH,
         )
         pl.when(owner != z)(copy.start)
@@ -357,8 +363,11 @@
         return ring_sum(
             lambda j, k: d_s[h, j, row_half(k, rx), lo:hi],
             lambda j, k: d_b.at[h, j, row_half(k, rx), lo:hi],
-            lambda k: d_far.at[h, k, :, lo:hi],
-            lambda s, k: d_near.at[h, s, k, :, lo:hi],
+            lambda k: d_far.at[h, :, :, lo:hi] if k is None else d_far.at[h, k, :, lo:hi],
+            lambda s, k: (
+                d_near.at[h, :, :, :, lo:hi] if s is None else d_near.at[h, s, k, :, lo:hi]
+            ),
+            d_b.at[h, 0:3, :, lo:hi],
             x, x_up, x_dn, x_far, lambda j: {"dp": j},
         )
 
@@ -375,8 +384,15 @@
                 d_s[h, j, :, start:stop] = rows
                 d_b[h, j, :, start:stop] = rows.astype(BF16)
 
-    out_pairs = [[sems.take() for _ in z_peers] for _ in cuts]
-    back_pairs = [[sems.take() for _ in z_peers] for _ in cuts]
+    def all_but_one(ref, i):
+        h, lo, hi = cuts[i]
+        return ref.at[h, 0 : n_z - 1, :, lo:hi]
+
+    out_pairs = [sems.take() for _ in cuts]
+    back_pairs = [sems.take() for _ in cuts]
+    for i in range(len(cuts)):
+        drains.append((all_but_one(zs_d, i), out_pairs[i]))
+        drains.append((all_but_one(po_d, i), back_pairs[i]))
 
     def down_scatter(i):
         h, lo, hi = cuts[i]
@@ -387,27 +403,25 @@
                 halves[k].reshape(per_half, -1, hi - lo).astype(BF16)
             )
         zr_d[h, z, :, lo:hi] = zs_d[h, z, :, lo:hi]
-        for p, pair in zip(z_peers, out_pairs[i]):
-            ship(zs_d.at[h, p, :, lo:hi], zr_d.at[h, z, :, lo:hi], {"mb": p}, pair)
+        for p in z_peers:
+            ship(zs_d.at[h, p, :, lo:hi], zr_d.at[h, z, :, lo:hi], {"mb": p}, out_pairs[i], False)
 
     def down_prefix(i):
         h, lo, hi = cuts[i]
-        for p, pair in zip(z_sources, out_pairs[i]):
-            arrive(zr_d.at[h, p, :, lo:hi], pair)
+        arrive(all_but_one(zr_d, i), out_pairs[i])
         total = zr_d[h, 0, :, lo:hi].astype(F32)
         po_d[h, 0, :, lo:hi] = total.astype(BF16)
         for p in range(1, n_z):
             total += zr_d[h, p, :, lo:hi].astype(F32)
             po_d[h, p, :, lo:hi] = total.astype(BF16)
         keep(po_d.at[h, z, :, lo:hi], rf_d.at[h, z, :, lo:hi])
-        for p, pair in zip(z_peers, back_pairs[i]):
-            ship(po_d.at[h, p, :, lo:hi], rf_d.at[h, z, :, lo:hi], {"mb": p}, pair)
+        for p in z_peers:
+            ship(po_d.at[h, p, :, lo:hi], rf_d.at[h, z, :, lo:hi], {"mb": p}, back_pairs[i], False)
 
     def down_arrive(i):
-        h, lo, hi = cuts[i]
-        for p, pair in zip(z_sources, back_pairs[i]):
-            arrive(rf_d.at[h, p, :, lo:hi], pair)
-
+        arrive(all_but_one(rf_d, i), back_pairs[i])
+
+    assert sems.used == [send.shape[0], recv.shape[0]], sems.used
     lat_gather.near()
     get_w[0].wait()
     get_g_other.wait()
@@ -439,37 +453,37 @@
     up_rings[1].second()
     up_total(0)
     lg_gathers[0].across_far()
-    up_swap()
+    up_swap(2)
     up_rings[2].far()
     up_rings[2].near()
     lg_gathers[0].across()
     up_total(1)
     get_h.wait()
     lg_gathers[0].finish(0, 1, 2, 3)
+    lg_gathers[1].across_far()
     down_part(0)
     down_rings[0].far()
     down_part(1)
     down_rings[1].far()
+    lg_gathers[1].across()
     up_rings[2].second()
     down_rings[0].near()
     down_rings[1].near()
     up_owner(0)
-    lg_gathers[1].across_far()
-    lg_gathers[1].across()
     lg_gathers[1].finish(0, 1, 2, 3)
+    lat_gather.across_halves()
     down_part(2)
     down_rings[2].far()
     down_part(3)
     down_rings[3].far()
-    up_owner(1)
+    lat_gather.finish(3)
+    up_part(3)
     down_rings[0].second()
     down_rings[1].second()
     down_rings[2].near()
     down_rings[3].near()
+    up_owner(1)
     up_owner(2)
-    lat_gather.across_halves()
-    lat_gather.finish(3)
-    up_part(3)
     down_rings[2].second()
     down_rings[3].second()
     up_rings[3].far()
@@ -492,6 +506,11 @@
     up_final()
     for copy in sent:
         copy.wait_send()
+    for whole, pair in drains:
+        pltpu.make_async_remote_copy(
+            src_ref=whole, dst_ref=whole, send_sem=pair[0], recv_sem=recv.at[0],
+            device_id={"tp": partner}, device_id_type=MESH,
+        ).wait_send()
     for copy in kept:
         copy.wait()
     for owner, copy, own in to_owner:
@@ -536,7 +555,8 @@
     up_shape = (n_z // 2, rows_u, columns)
     down_shape = (NH, n_z, rx // n_z, width)
     in_hbm = pl.BlockSpec(memory_space=pltpu.HBM)
-    n_sems = 8 + NH + 3 * NH + 8 * NH + 8 * NG + (n_z // 2 - 1) + 2 * (6 + 2 * (n_z - 1)) * NH
+    both = 8 + NH + 3 * NH + 8 * NH + 2 * NG + (n_z // 2 - 1) + 2 * 2 * NH
+    n_send, n_recv = both + NG + 2 * NH, both + 2 * NG + 2 * 2 * NH
     up_grad, running = pl.pallas_call(
         functools.partial(kernel, n_z, n_y, n_x),
         out_shape=(
@@ -567,17 +587,17 @@
             pltpu.VMEM(down_shape, BF16),
             pltpu.VMEM(down_shape, BF16),
             pltpu.VMEM((NG, n_x, 2, rows_u, columns), BF16),
-            pltpu.VMEM((2, n_x, rows_u, columns // 2), BF16),
-            pltpu.VMEM((n_x, rows_u, columns), BF16),
+            pltpu.VMEM((len(SWAPPED), 2, n_x, rows_u, columns // 2), BF16),
+            pltpu.VMEM((len(SWAPPED), n_x, rows_u, columns), BF16),
             pltpu.VMEM((NG, 2, 2, rows_u, columns // 2), BF16),
             pltpu.VMEM((NG, 2, 2, 2, rows_u, columns // 2), BF16),
             pltpu.VMEM((NG, 2, rows_u, columns), BF16),
             pltpu.VMEM((NG, 2, rows_u, columns // 2), BF16),
             pltpu.VMEM((n_y, rows_u, columns), BF16),
-            pltpu.SemaphoreType.DMA((10,)),
+            pltpu.SemaphoreType.DMA((6 + NH,)),
             pltpu.SemaphoreType.DMA((2 * NH + NG,)),
-            pltpu.SemaphoreType.DMA((n_sems,)),
-            pltpu.SemaphoreType.DMA((n_sems,)),
+            pltpu.SemaphoreType.DMA((n_send,)),
+            pltpu.SemaphoreType.DMA((n_recv,)),
         ],
         compiler_params=pltpu.CompilerParams(
             collective_id=0, has_side_effects=True, vmem_limit_bytes=66_400_000

time: 56.3 us -> 54.5 us (0.968); the launches traced: 55.4 us -> 54.4 us
  Pallas kernels: 54.8 us -> 53.8 us
    pallas_call x1, Pallas kernels: 52.9 us -> 51.9 us  [local(): pl.pallas_call(functools.partial(kernel, n_z, n_y, n_x), out_shape=(jax.S...]
where the time goes in v4:
time: 54.5 us; the launch traced here: 54.4 us
  Pallas kernels  53.8 us (99%)
  between operations  0.64 us (1%)
    pallas_call x1, Pallas kernels, local(): pl.pallas_call(functools.partial(kernel, n_z, n_y, n_x), out_shape=(jax.S...  51.9 us
    pallas_call x1, Pallas kernels, local(): pl.pallas_call(finish_kernel, out_shape=(jax.ShapeDtypeStruct((rows_u, co...  1.92 us

profile of v4, /device:TPU:16, one launch (start us, length us, event | category | flops | bytes accessed | tf_op | source)
XLA Modules:
  0.0 54.4 jit_solution(6225353138490147301)
XLA Ops:
  0.6 51.9 %shard_map.77 = (bf16[4,16,2048]{2,1,0:T(8,128)(2,1)}, bf16[2,8,8,896]{3,2,1,0:T(8,128)(2,1)}) custom-call(bf16[1024,896]{1,0:T(8,128)(2,1)} %bitcast.9, bf16[2,64,512]{2,1,0:T(8,128)(2,1)} %bitcast.10, bf16[2,512,2048]{2,1,0:T(8,128)(2,1)} %bitcast.7, bf16[4,2,64,2048]{3,2,1,0:T(8,128)(2,1)} %bitcast.8, s32[1,16]{1,0:T(1,128)} %tokens_in.1, s32[1,2]{1,0:T(1,128)} %slots_in.1), custom_call_target="tpu_custom_call" | custom-call | tf_op jit(solution)/shard_map/pallas_call | solution.py:560
  52.5 1.9 %shard_map.78 = (f32[16,2048]{1,0:T(8,128)}, f32[896,128]{1,0:T(8,128)}) custom-call(bf16[4,16,2048]{2,1,0:T(8,128)(2,1)} %get-tuple-element.6.up_in, bf16[2,8,8,896]{3,2,1,0:T(8,128)(2,1)} %get-tuple-element.7.down_in), custom_call_target="tpu_custom_call" | custom-call | tf_op jit(solution)/shard_map/pallas_call | solution.py:613

commit v5 on v4

--- a/solution.py
+++ b/solution.py
@@ -139,35 +139,37 @@
     def row_half(k, rows):
         return pl.ds(k * rows // 2, rows // 2)
 
-    def gather(block, half):
-        pairs = [sems.take() for _ in range(8)]
+    def gather(block, half, seven):
+        out = sems.take(1, 0)
+        drains.append((seven, out))
+        pairs = [(out[0], sems.take(0, 1)[1]) for _ in range(8)]
 
         def near():
-            ship(block(tp), block(tp), {"tp": y_up}, pairs[0])
-            ship(block(tp), block(tp), {"tp": y_dn}, pairs[1])
-            ship(block(tp), block(tp), {"tp": partner}, pairs[2])
+            ship(block(tp), block(tp), {"tp": y_up}, pairs[0], False)
+            ship(block(tp), block(tp), {"tp": y_dn}, pairs[1], False)
+            ship(block(tp), block(tp), {"tp": partner}, pairs[2], False)
 
         def across():
             arrive(block(y_dn), pairs[0])
-            ship(block(y_dn), block(y_dn), {"tp": partner}, pairs[5])
+            ship(block(y_dn), block(y_dn), {"tp": partner}, pairs[5], False)
             arrive(block(y_up), pairs[1])
-            ship(block(y_up), block(y_up), {"tp": partner}, pairs[6])
+            ship(block(y_up), block(y_up), {"tp": partner}, pairs[6], False)
 
         def along():
-            ship(half(y_dn, 0), half(y_dn, 0), {"tp": y_up}, pairs[3])
-            ship(half(y_up, 1), half(y_up, 1), {"tp": y_dn}, pairs[4])
+            ship(half(y_dn, 0), half(y_dn, 0), {"tp": y_up}, pairs[3], False)
+            ship(half(y_up, 1), half(y_up, 1), {"tp": y_dn}, pairs[4], False)
 
         def across_halves():
             arrive(half(y_far, 0), pairs[3])
             arrive(half(y_far, 1), pairs[4])
-            ship(block(y_far), block(y_far), {"tp": partner}, pairs[7])
+            ship(block(y_far), block(y_far), {"tp": partner}, pairs[7], False)
 
         def far():
-            ship(block(tp), block(tp), {"tp": y_far}, pairs[3])
+            ship(block(tp), block(tp), {"tp": y_far}, pairs[3], False)
 
         def across_far():
             arrive(block(y_far), pairs[3])
-            ship(block(y_far), block(y_far), {"tp": partner}, pairs[7])
+            ship(block(y_far), block(y_far), {"tp": partner}, pairs[7], False)
 
         def finish(*which):
             for k in which:
@@ -207,6 +209,7 @@
     lat_gather = gather(
         lambda i: lat_all.at[i],
         lambda i, k: lat_all.at[i, row_half(k, n_lat)],
+        lat_all.at[0:7],
     )
 
     pair_pairs = [sems.take() for _ in range(NH)]
@@ -246,6 +249,7 @@
         return gather(
             lambda i: lg_all.at[h, :, columns_of(i)],
             lambda i, k: lg_all.at[h, row_half(k, rows_h), columns_of(i)],
+            lg_all.at[h, :, 0 : 7 * blk],
         )
 
     lg_gathers = [lg_gather(h) for h in range(NH)]
@@ -556,7 +560,7 @@
     down_shape = (NH, n_z, rx // n_z, width)
     in_hbm = pl.BlockSpec(memory_space=pltpu.HBM)
     both = 8 + NH + 3 * NH + 8 * NH + 2 * NG + (n_z // 2 - 1) + 2 * 2 * NH
-    n_send, n_recv = both + NG + 2 * NH, both + 2 * NG + 2 * 2 * NH
+    n_send, n_recv = both - 7 - 7 * NH + NG + 2 * NH, both + 2 * NG + 2 * 2 * NH
     up_grad, running = pl.pallas_call(
         functools.partial(kernel, n_z, n_y, n_x),
         out_shape=(

time: 54.5 us -> 54.3 us (level)
  no operation moved by 1% of the time
where the time goes in v5:
time: 54.3 us; the launch traced here: 54.2 us
  Pallas kernels  53.5 us (99%)
  between operations  0.64 us (1%)
    pallas_call x1, Pallas kernels, local(): pl.pallas_call(functools.partial(kernel, n_z, n_y, n_x), out_shape=(jax.S...  51.6 us
    pallas_call x1, Pallas kernels, local(): pl.pallas_call(finish_kernel, out_shape=(jax.ShapeDtypeStruct((rows_u, co...  1.92 us

profile of v5, /device:TPU:16, one launch (start us, length us, event | category | flops | bytes accessed | tf_op | source)
XLA Modules:
  0.0 54.2 jit_solution(14371186609950251861)
XLA Ops:
  0.6 51.6 %shard_map.77 = (bf16[4,16,2048]{2,1,0:T(8,128)(2,1)}, bf16[2,8,8,896]{3,2,1,0:T(8,128)(2,1)}) custom-call(bf16[1024,896]{1,0:T(8,128)(2,1)} %bitcast.9, bf16[2,64,512]{2,1,0:T(8,128)(2,1)} %bitcast.10, bf16[2,512,2048]{2,1,0:T(8,128)(2,1)} %bitcast.7, bf16[4,2,64,2048]{3,2,1,0:T(8,128)(2,1)} %bitcast.8, s32[1,16]{1,0:T(1,128)} %tokens_in.1, s32[1,2]{1,0:T(1,128)} %slots_in.1), custom_call_target="tpu_custom_call" | custom-call | tf_op jit(solution)/shard_map/pallas_call | solution.py:564
  52.3 1.9 %shard_map.78 = (f32[16,2048]{1,0:T(8,128)}, f32[896,128]{1,0:T(8,128)}) custom-call(bf16[4,16,2048]{2,1,0:T(8,128)(2,1)} %get-tuple-element.6.up_in, bf16[2,8,8,896]{3,2,1,0:T(8,128)(2,1)} %get-tuple-element.7.down_in), custom_call_target="tpu_custom_call" | custom-call | tf_op jit(solution)/shard_map/pallas_call | solution.py:617
